TPU v7x, 512 devices: a whole 4x4x16 slice. The times are simulated.
512 devices in a mesh: ctx: 64 (over y, z), head: 8 (over x, core).
Axes of the slice: x: 4, y: 4, z: 16, core: 2. Of those that a mesh axis runs over, the one named last changes fastest.
Arguments:
- queries: bfloat16 [32768, 16, 128], P('ctx', 'head'), may hold values from -130 to 130, as said below
- values: bfloat16 [32768, 16, 128], P('ctx', 'head'), may hold values from -6 to 6
- codes: int32 [32768, 16], P('ctx', 'head'), may hold values from 0 to 511
- codebook: bfloat16 [16, 512, 128], P('head'), may hold values from -8 to 8, as said below
- out_weight: bfloat16 [2048, 2048], P('head'), may hold values from -0.1875 to 0.1875
Outputs:
- mixed: bfloat16 [32768, 2048], P('ctx', 'head')
Inputs may be any that keep to these rules, and one draw needn't show every extreme that they name: `queries`: every entry has magnitude at most 130. `codebook`: every entry has magnitude at most 8.
All inputs are finite; a program needn't handle non-finite values.
Results may differ from a plain program's by a relative error of at most 0.0066.
Values may be sent and summed in bfloat16 or wider, within the bound.
A program may use at most 64 MiB of HBM per device.

v0:
```python
import jax
import jax.numpy as jnp
from jax import lax
from jax.sharding import Mesh
from jax.sharding import PartitionSpec as P

BLOCK = 512
CTX = ("ctx_0", "ctx_1")


def from_behind(value, axis, steps):
    count = lax.axis_size(axis)
    first, last = (max(0, -steps), min(count, count - steps))
    return lax.ppermute(value, axis, [(source, source + steps) for source in range(first, last)])


def neutral_like(x, identity):
    return jax.tree.map(
        lambda part, zero: jnp.zeros_like(part) + jnp.asarray(zero, part.dtype), x, identity
    )


def prefix_by_axis(x, axes, combine, identity):
    before = start = neutral_like(x, identity)
    so_far = x
    for axis in reversed(axes):
        devices, here = (lax.axis_size(axis), lax.axis_index(axis))
        pieces = jax.tree.map(
            lambda part, kind: lax.all_gather(part.astype(kind), axis),
            so_far,
            (jnp.bfloat16, jnp.bfloat16),
        )
        inside, so_far = (start, start)
        for k in range(devices):
            passed = k < here
            so_far = combine(
                so_far, jax.tree.map(lambda part, own: part[k].astype(own.dtype), pieces, x)
            )
            inside = jax.tree.map(lambda new, old: jnp.where(passed, new, old), so_far, inside)
        before = combine(inside, before)
    return before


def laid_out(parts, dim):
    parts = jnp.moveaxis(parts, 0, dim)
    lengths = parts.shape
    return parts.reshape(*lengths[:dim], lengths[dim] * lengths[dim + 1], *lengths[dim + 2 :])


def sent_to_all(x, axis):
    copies = jnp.broadcast_to(x, (lax.axis_size(axis), *x.shape))
    return lax.all_to_all(copies, axis, split_axis=0, concat_axis=0, tiled=True)


def gathered_copies(x, axis, dim):
    return laid_out(sent_to_all(x, axis), dim)


def attend(query, cur_keys, cur_values, prev_keys, prev_values, live, book, cache_sum, cache_count):
    scale = query.shape[-1] ** (-0.5)
    code_scores = jnp.dot(query, book.T, preferred_element_type=jnp.float32) * scale
    cur_scores = jnp.dot(query, cur_keys.T, preferred_element_type=jnp.float32) * scale
    prev_scores = jnp.dot(query, prev_keys.T, preferred_element_type=jnp.float32) * scale
    rows = lax.broadcasted_iota(jnp.int32, cur_scores.shape, 0)
    cols = lax.broadcasted_iota(jnp.int32, cur_scores.shape, 1)
    causal = rows >= cols
    present = (cache_count > 0.0)[None, :]
    top = jnp.max(jnp.where(causal, cur_scores, -jnp.inf), axis=1)
    top = jnp.maximum(top, jnp.max(jnp.where(live, prev_scores, -jnp.inf), axis=1))
    top = jnp.maximum(top, jnp.max(jnp.where(present, code_scores, -jnp.inf), axis=1))
    top = top[:, None]
    cur_weight = jnp.where(causal, jnp.exp(cur_scores - top), 0.0)
    prev_weight = jnp.where(live, jnp.exp(prev_scores - top), 0.0)
    code_weight = jnp.where(present, jnp.exp(code_scores - top), 0.0)
    denom = (
        jnp.sum(cur_weight, axis=1)
        + jnp.sum(prev_weight, axis=1)
        + jnp.sum(code_weight * cache_count[None, :], axis=1)
    )
    numer = jnp.dot(cur_weight.astype(jnp.bfloat16), cur_values, preferred_element_type=jnp.float32)
    numer = numer + jnp.dot(
        prev_weight.astype(jnp.bfloat16), prev_values, preferred_element_type=jnp.float32
    )
    numer = numer + jnp.dot(code_weight, cache_sum, precision=lax.Precision.HIGHEST)
    return (numer / denom[:, None]).astype(jnp.bfloat16)


def add_totals(earlier, later):
    return (earlier[0] + later[0], earlier[1] + later[1])


def on_device(queries, values, codes, codebook, out_weight):
    tokens, local_heads, width = queries.shape
    ncodes = codebook.shape[1]
    nblocks = tokens // BLOCK
    keys = jax.vmap(lambda book, index: book[index], in_axes=(0, 1), out_axes=1)(codebook, codes)
    table = lax.broadcasted_iota(jnp.int32, (1, 1, ncodes), 2)
    onehot = (
        (codes[:, :, None] == table)
        .astype(jnp.bfloat16)
        .reshape(nblocks, BLOCK, local_heads, ncodes)
    )
    block_sums = jnp.einsum(
        "bths,bthd->bhsd",
        onehot,
        values.reshape(nblocks, BLOCK, local_heads, width),
        preferred_element_type=jnp.float32,
    )
    block_counts = jnp.sum(onehot.astype(jnp.float32), axis=1)
    last_sum, last_count = (block_sums[nblocks - 1], block_counts[nblocks - 1])
    rest_sum = jnp.sum(block_sums[: nblocks - 1], axis=0)
    rest_count = jnp.sum(block_counts[: nblocks - 1], axis=0)
    prev_keys, prev_values = from_behind((keys, values), CTX, 1)
    zero_sum = jnp.zeros_like(last_sum)
    zero_count = jnp.zeros_like(last_count)
    total_sum, total_count = prefix_by_axis(
        (rest_sum + last_sum, rest_count + last_count), CTX, add_totals, (zero_sum, zero_count)
    )
    pend_sum, pend_count = (
        from_behind(last_sum.astype(jnp.bfloat16), CTX, 1).astype(last_sum.dtype),
        from_behind(last_count.astype(jnp.bfloat16), CTX, 1).astype(last_count.dtype),
    )
    cache_sum = total_sum - pend_sum
    cache_count = total_count - pend_count
    live = lax.axis_index(CTX) > 0
    attended = jax.vmap(attend, in_axes=(1, 1, 1, 1, 1, None, 0, 0, 0), out_axes=1)(
        queries, keys, values, prev_keys, prev_values, live, codebook, cache_sum, cache_count
    )
    attended_all = attended.reshape(tokens, local_heads * width)
    columns = lax.all_to_all(out_weight, "head", split_axis=1, concat_axis=0, tiled=True)
    summed = jnp.dot(
        gathered_copies(attended_all, "head", 1), columns, preferred_element_type=jnp.float32
    )
    return summed.astype(jnp.bfloat16)


def solution(mesh):
    finer = Mesh(mesh.devices.reshape(4, 16, mesh.shape["head"]), ("ctx_0", "ctx_1", "head"))
    placed = (
        P(CTX, "head", None),
        P(CTX, "head", None),
        P(CTX, "head"),
        P("head", None, None),
        P("head", None),
    )
    return jax.shard_map(
        on_device, mesh=finer, in_specs=placed, out_specs=P(CTX, "head"), check_vma=False
    )
```

profile of v0, /device:TPU:1, one launch (start us, length us, event | category | flops | bytes accessed | tf_op | source)
XLA Modules:
  0.0 175.7 jit_solution(5980455730534582774)
XLA Ops:
  6.5 1.2 copy.55
  7.7 1.9 %fusion.19 = bf16[2,512,128]{2,1,0:T(8,128)(2,1)} fusion(bf16[512,2,128]{0,2,1:T(8,128)(2,1)S(1)} %copy.55, s32[512,2]{0,1:T(2,128)} %param.7), kind=kOutput, calls=%fused_computation.28 | convolution fusion | flops 134873088 | bytes 528384 | tf_op jit(solution)/shard_map/bths,bthd->bhsd/dot_general | solution.py:103
  9.7 0.0 all-gather.8.cloned.1.call-update
  9.7 5.1 %collective-permute-start.3 = (bf16[2,512,128]{2,1,0:T(8,128)(2,1)}, bf16[2,512,128]{2,1,0:T(8,128)(2,1)}, u32[]{:S(2)}, u32[]{:S(2)}) collective-permute-start(bf16[2,512,128]{2,1,0:T(8,128)(2,1)} %fusion.19), channel_id=1, source_target_pairs={{0,8},{8,16},{16,24},{24,32},{32,40},{40,48},{48,56},{56,64},{64,7... | collective-permute-start | bytes 786440 | tf_op jit(solution)/shard_map/ppermute | solution.py:14
  14.8 3.5 %collective-permute-start.2 = (bf16[512,2,128]{0,2,1:T(8,128)(2,1)S(1)}, bf16[512,2,128]{0,2,1:T(8,128)(2,1)}, u32[]{:S(2)}, u32[]{:S(2)}) collective-permute-start(bf16[512,2,128]{0,2,1:T(8,128)(2,1)S(1)} %copy.55), channel_id=1, source_target_pairs={{0,8},{8,16},{16,24},{24,32},{32,40},{40,48},{48,56},{56,64},{64,7... | collective-permute-start | bytes 786440 | tf_op jit(solution)/shard_map/ppermute | solution.py:14
  18.3 1.0 fusion.23
  19.3 2.9 %collective-permute-start.1 = (bf16[2,512]{1,0:T(2,128)(2,1)S(1)}, bf16[2,512]{1,0:T(2,128)(2,1)S(1)}, u32[]{:S(2)}, u32[]{:S(2)}) collective-permute-start(bf16[2,512]{1,0:T(2,128)(2,1)S(1)} %fusion.23), channel_id=1, source_target_pairs={{0,8},{8,16},{16,24},{24,32},{32,40},{40,48},{48,56},{56,64},{64,7... | collective-permute-start | bytes 6152 | tf_op jit(solution)/shard_map/ppermute | solution.py:14
  22.2 10.5 %gather_fusion = bf16[1024,128]{1,0:T(8,128)(2,1)} fusion(bf16[2,512,128]{2,1,0:T(8,128)(2,1)S(1)} %copy-done, s32[1024]{0:T(1024)S(1)} %bitcast.324), kind=kCustom, calls=%fused_computation | custom fusion | bytes 532480 | tf_op jit(solution)/shard_map/vmap()/gather | solution.py:96
  32.7 4.8 %collective-permute-start = (bf16[512,2,128]{2,0,1:T(8,128)(2,1)}, bf16[512,2,128]{2,0,1:T(8,128)(2,1)S(1)}, u32[]{:S(2)}, u32[]{:S(2)}) collective-permute-start(bf16[512,2,128]{2,0,1:T(8,128)(2,1)} %bitcast.4), channel_id=1, source_target_pairs={{0,8},{8,16},{16,24},{24,32},{32,40},{40,48},{48,56},{56,64},{64,7... | collective-permute-start | bytes 786440 | tf_op jit(solution)/shard_map/ppermute | solution.py:14
  37.5 0.5 copy.61
  38.0 1.3 copy.62
  39.3 6.1 %all-to-all-start.1 = ((bf16[256,8,256]{2,0,1:T(8,128)(2,1)}), bf16[256,8,256]{2,0,1:T(8,128)(2,1)}, u32[]{:S(2)}, u32[]{:S(2)}) async-start(bf16[256,8,256]{2,0,1:T(8,128)(2,1)} %copy.62), calls=%async_computation.1 | async-start | bytes 2097152 | tf_op jit(solution)/shard_map/all_to_all | solution.py:130
  45.4 25.6 %all-gather.2 = bf16[16,2,512]{2,1,0:T(2,128)(2,1)S(1)} all-gather(bf16[1,2,512]{2,1,0:T(2,128)(2,1)S(1)} %bitcast.327), channel_id=2, replica_groups=mesh['ctx_0'=4,'ctx_1'=16,'head'=8] {'ctx_1'}, dimensions={0}, use_global_device_ids=true | all-gather | bytes 34816 | tf_op jit(solution)/shard_map/all_gather | solution.py:29
  71.1 0.1 iota_compare_fusion.5
  71.2 2.8 %fusion.2 = (f32[2,512]{1,0:T(2,128)S(1)}, f32[2,512,512]{2,1,0:T(8,128)}) fusion(pred[512,512]{0,1:T(8,128)(4,1)S(1)} %iota_compare_fusion.5, bf16[2,512,128]{2,1,0:T(8,128)(2,1)} %bitcast.2, bf16[512,2,128]{2,1,0:T(2,128)(2,1)S(1)} %copy-done.4), kind=kOutput, calls=%fused_computation.7 | convolution fusion | flops 135789568 | bytes 2887680 | tf_op jit(solution)/shard_map/vmap()/dot_general | solution.py:62
  74.0 9.3 %all_gather.17 = bf16[4,2,512]{2,1,0:T(2,128)(2,1)S(1)} all-gather(bf16[1,2,512]{2,1,0:T(2,128)(2,1)S(1)} %fusion.156), channel_id=1, replica_groups=mesh['ctx_0'=4,'ctx_1'=16,'head'=8] {'ctx_0'}, dimensions={0}, use_global_device_ids=true | all-gather | bytes 10240 | tf_op jit(solution)/shard_map/all_gather | solution.py:29
  83.3 0.1 broadcast_compare_fusion
  83.4 0.7 select_reduce_fusion
  84.1 5.3 %all-gather.8.cloned.1.call-done = bf16[32,512,128]{2,1,0:T(8,128)(2,1)} async-done(((bf16[2,512,128]{2,1,0:T(8,128)(2,1)}), bf16[32,512,128]{2,1,0:T(8,128)(2,1)}) %all-gather.8.cloned.1.call-update) | async-done | bytes 4194320 | tf_op jit(solution)/shard_map/all_gather | solution.py:29
  89.3 3.4 %fusion.70 = bf16[1,2,512,128]{3,2,1,0:T(8,128)(2,1)} fusion(bf16[32,512,128]{2,1,0:T(8,128)(2,1)} %all-gather.8.cloned.1.call-done), kind=kLoop, calls=%fused_computation.95 | loop fusion | flops 4194304 | bytes 4456448 | tf_op jit(solution)/shard_map/convert_element_type | solution.py:29
  92.8 0.5 select_reduce_fusion.1
  93.3 1.2 copy-done.3
  94.5 1.5 fusion.21
  96.0 1.1 fusion.8
  97.1 0.6 bitcast_reduce_fusion
  97.7 28.2 %all-gather.6.cloned.1.call-done = bf16[4,2,512,128]{3,2,1,0:T(8,128)(2,1)} async-done(((bf16[1,2,512,128]{3,2,1,0:T(8,128)(2,1)}), bf16[4,2,512,128]{3,2,1,0:T(8,128)(2,1)}) %all-gather.6.cloned.1.call-update) | async-done | bytes 1048592 | tf_op jit(solution)/shard_map/all_gather | solution.py:29
  125.9 5.2 %fusion.7 = f32[2,512,128]{1,2,0:T(8,128)S(1)} fusion(f32[2,512,512]{1,2,0:T(8,128)S(1)} %get-tuple-element.10, f32[2,512]{1,0:T(2,128)S(1)} %maximum_maximum_fusion, pred[2,512]{1,0:T(4,128)(4,1)S(1)} %get-tuple-element.7, bf16[2,512,128]{2,1,0:T(8,128)(2,1)} %collective-permute-done.3, bf16[4,2,512,128]{3,2,1,0:T(8,128)(2,1)} %all-gather.6.cloned.1.call-done, ...), kind=kOutput, calls=%fused_computation.19 | convolution fusion | flops 814874624 | bytes 8131604 | tf_op jit(solution)/shard_map/vmap()/dot_general | solution.py:84
  131.1 1.8 %fusion.20 = bf16[512,2,128]{0,2,1:T(8,128)(2,1)S(1)} fusion(f32[2,512,128]{1,2,0:T(8,128)S(1)} %fusion.7, f32[2,512,128]{1,2,0:T(8,128)} %fusion.21, bf16[512,2,128]{0,2,1:T(8,128)(2,1)} %collective-permute-done.2, f32[2,512,512]{1,2,0:T(8,128)S(1)} %copy-done.2, f32[2,512]{1,0:T(2,128)S(1)} %maximum_maximum_fusion, pred[]{:T(512)S(6)} %gt.66, ...), kind=kOutput, calls=%fused_computation.29 | convolution fusion | flops 136839168 | bytes 3678209 | tf_op jit(solution)/shard_map/vmap()/dot_general | solution.py:81
  132.9 0.1 copy.60
  133.1 0.1 broadcast_in_dim.51
  133.2 33.0 %all_to_all.21 = bf16[8,512,256]{2,1,0:T(8,128)(2,1)S(1)} all-to-all(bf16[8,512,256]{2,1,0:T(8,128)(2,1)S(1)} %broadcast_in_dim.51), channel_id=1, replica_groups=mesh['ctx_0'=4,'ctx_1'=16,'head'=8] {'head'}, dimensions={0} | all-to-all | bytes 4194304 | tf_op jit(solution)/shard_map/all_to_all | solution.py:52
  166.2 2.6 %fusion.16 = bf16[512,256]{1,0:T(8,128)(2,1)} fusion(bf16[8,512,256]{2,1,0:T(8,128)(2,1)S(1)} %all_to_all.21, bf16[256,8,256]{2,0,1:T(8,128)(2,1)} %all-to-all-done.1), kind=kOutput, calls=%fused_computation.27 | convolution fusion | flops 537001984 | bytes 3407872 | tf_op jit(solution)/shard_map/dot_general | solution.py:131
  (26 shorter events, 0.1 us)
Async XLA Ops:
  6.5 15.6 %copy-start = (bf16[2,512,128]{2,1,0:T(8,128)(2,1)S(1)}, bf16[2,512,128]{2,1,0:T(8,128)(2,1)}, u32[]{:S(2)}) copy-start(bf16[2,512,128]{2,1,0:T(8,128)(2,1)} %param.8) | copy-start | bytes 786436
  6.5 15.6 %copy-start.6 = (s32[512,2]{0,1:T(2,128)S(1)}, s32[512,2]{0,1:T(2,128)}, u32[]{:S(2)}) copy-start(s32[512,2]{0,1:T(2,128)} %param.7) | copy-start | bytes 12292
  6.5 82.8 %all-gather.8.cloned.1.call-start = ((), (), s32[]{:S(2)}) async-start(), calls=%async_computation.3 | async-start | bytes 4456448 | tf_op jit(solution)/shard_map/all_gather | solution.py:29
  7.7 29.8 %copy-start.5 = (bf16[256,2048]{1,0:T(8,128)(2,1)S(1)}, bf16[256,2048]{1,0:T(8,128)(2,1)}, u32[]{:S(2)}) copy-start(bf16[256,2048]{1,0:T(8,128)(2,1)} %param.9) | copy-start | bytes 3145732
  9.7 88.0 %collective-permute-start.3 = (bf16[2,512,128]{2,1,0:T(8,128)(2,1)}, bf16[2,512,128]{2,1,0:T(8,128)(2,1)}, u32[]{:S(2)}, u32[]{:S(2)}) collective-permute-start(bf16[2,512,128]{2,1,0:T(8,128)(2,1)} %fusion.19), channel_id=1, source_target_pairs={{0,8},{8,16},{16,24},{24,32},{32,40},{40,48},{48,56},{56,64},{64,7... | collective-permute-start | bytes 786440 | tf_op jit(solution)/shard_map/ppermute | solution.py:14
  14.8 116.4 %collective-permute-start.2 = (bf16[512,2,128]{0,2,1:T(8,128)(2,1)S(1)}, bf16[512,2,128]{0,2,1:T(8,128)(2,1)}, u32[]{:S(2)}, u32[]{:S(2)}) collective-permute-start(bf16[512,2,128]{0,2,1:T(8,128)(2,1)S(1)} %copy.55), channel_id=1, source_target_pairs={{0,8},{8,16},{16,24},{24,32},{32,40},{40,48},{48,56},{56,64},{64,7... | collective-permute-start | bytes 786440 | tf_op jit(solution)/shard_map/ppermute | solution.py:14
  19.3 64.0 %collective-permute-start.1 = (bf16[2,512]{1,0:T(2,128)(2,1)S(1)}, bf16[2,512]{1,0:T(2,128)(2,1)S(1)}, u32[]{:S(2)}, u32[]{:S(2)}) collective-permute-start(bf16[2,512]{1,0:T(2,128)(2,1)S(1)} %fusion.23), channel_id=1, source_target_pairs={{0,8},{8,16},{16,24},{24,32},{32,40},{40,48},{48,56},{56,64},{64,7... | collective-permute-start | bytes 6152 | tf_op jit(solution)/shard_map/ppermute | solution.py:14
  32.7 60.0 %collective-permute-start = (bf16[512,2,128]{2,0,1:T(8,128)(2,1)}, bf16[512,2,128]{2,0,1:T(8,128)(2,1)S(1)}, u32[]{:S(2)}, u32[]{:S(2)}) collective-permute-start(bf16[512,2,128]{2,0,1:T(8,128)(2,1)} %bitcast.4), channel_id=1, source_target_pairs={{0,8},{8,16},{16,24},{24,32},{32,40},{40,48},{48,56},{56,64},{64,7... | collective-permute-start | bytes 786440 | tf_op jit(solution)/shard_map/ppermute | solution.py:14
  38.0 33.1 %copy-start.4 = (bf16[512,2,128]{2,1,0:T(2,128)(2,1)S(1)}, bf16[512,2,128]{2,1,0:T(2,128)(2,1)}, u32[]{:S(2)}) copy-start(bf16[512,2,128]{2,1,0:T(2,128)(2,1)} %param.5) | copy-start | bytes 786436
  39.3 93.7 %all-to-all-start.1 = ((bf16[256,8,256]{2,0,1:T(8,128)(2,1)}), bf16[256,8,256]{2,0,1:T(8,128)(2,1)}, u32[]{:S(2)}, u32[]{:S(2)}) async-start(bf16[256,8,256]{2,0,1:T(8,128)(2,1)} %copy.62), calls=%async_computation.1 | async-start | bytes 2097152 | tf_op jit(solution)/shard_map/all_to_all | solution.py:130
  45.4 80.5 %all-gather.6.cloned.1.call-start = ((), (), s32[]{:S(2)}) async-start(), calls=%async_computation.2 | async-start | bytes 1310720 | tf_op jit(solution)/shard_map/all_gather | solution.py:29
  92.7 1.8 %copy-start.3 = (f32[2,512,512]{2,1,0:T(8,128)S(1)}, f32[2,512,512]{2,1,0:T(8,128)}, u32[]{:S(2)}) copy-start(f32[2,512,512]{2,1,0:T(8,128)} %get-tuple-element.12) | copy-start | bytes 6291460
  93.3 3.8 %copy-start.1 = (f32[2,512,512]{1,2,0:T(8,128)}, f32[2,512,512]{1,2,0:T(8,128)S(1)}, u32[]{:S(2)}) copy-start(f32[2,512,512]{1,2,0:T(8,128)S(1)} %get-tuple-element.14) | copy-start | bytes 6291460
  125.9 5.2 %copy-start.2 = (f32[2,512,512]{1,2,0:T(8,128)S(1)}, f32[2,512,512]{1,2,0:T(8,128)}, u32[]{:S(2)}) copy-start(f32[2,512,512]{1,2,0:T(8,128)} %copy-done.1) | copy-start | bytes 6291460
Sparse Core Ops, SparseCore 0:
  9.8 79.4 all-gather.7
  92.9 33.0 all-gather.5
where the time goes:
time: 176 us
  blocking collectives  67.9 us (39%)
  waiting for transfers between devices  33.5 us (19%)
  starting transfers between devices  22.3 us (13%)
  matrix products  17.1 us (10%)
  local copies, waits for them, and re-layouts  15 us (9%)
  between operations  13.6 us (8%)
  other arithmetic  6.21 us (4%)
    all_gather x2, blocking collectives, prefix_by_axis(): lax.all_gather(part.astype(kind), axis)  34.9 us
    all_gather x2, waiting for transfers between devices, prefix_by_axis(): lax.all_gather(part.astype(kind), axis)  33.5 us
    all_to_all x1, blocking collectives, sent_to_all(): return lax.all_to_all(copies, axis, split_axis=0, concat_axis=0, tiled=True)  33 us
    ppermute x4, starting transfers between devices, from_behind(): lax.ppermute(value, axis, [(source, source + steps) for source in range(f...  16.2 us
    gather x1, local copies, waits for them, and re-layouts, on_device(): book[index]  10.5 us
    all_to_all x1, starting transfers between devices, on_device(): lax.all_to_all(out_weight, 'head', split_axis=1, concat_axis=0, tiled=True)  6.09 us
    dot_general x1, matrix products, attend(): jnp.dot(code_weight, cache_sum, precision=lax.Precision.HIGHEST)  5.19 us
  transfers between devices with their start and end apart: 7, of which 2 were waited for; matrix products, arithmetic and copies ran while one was open for 18% of the time, Pallas kernels for 0%

commit v1 on v0

v1 whole, which is shorter than its diff:
```python
import functools

import jax
import jax.numpy as jnp
from jax import lax
from jax.experimental import pallas as pl
from jax.experimental.pallas import tpu as pltpu
from jax.sharding import Mesh
from jax.sharding import PartitionSpec as P

MESH = pl.DeviceIdType.MESH
CTX = ("y", "z")
HEAD = ("x", "c")
F32 = jnp.float32
BF16 = jnp.bfloat16
NEG = float("-inf")


def dot_nt(a, b):
    return lax.dot_general(a, b, (((1,), (1,)), ((), ())), preferred_element_type=F32)


def dot_nn(a, b, precision=None):
    return lax.dot_general(
        a, b, (((1,), (0,)), ((), ())), precision=precision, preferred_element_type=F32
    )


def wait_bytes(ref, sem):
    pltpu.make_async_copy(ref, ref, sem).wait()


def kernel(
    q_ref, v_ref, col_ref, row_ref, book_ref, w_ref, out_ref,
    sums, raw, tot_s, tot_r, pre_s, cache,
    csums, craw, ctot_s, ctot_r, cpre_s, ccache,
    code_sc, fw, aloc, stat, gath, wcol,
    z_send, z_recv, y_send, y_recv, w_send, w_recv, w_local, g_send, g_recv,
    *, ny, nz, nx,
):
    heads, tokens, width = q_ref.shape
    ncodes = book_ref.shape[1]
    sl = ncodes // nz
    half = tokens // 2
    cols = out_ref.shape[1]
    y, z, x, c = (lax.axis_index(name) for name in ("y", "z", "x", "c"))

    def far_first(j):
        step = (j + 1) // 2
        sign = 1 - 2 * lax.rem(j, 2)
        return lax.rem(z + nz // 2 + sign * step + nz, nz)

    def x_at(d):
        return lax.rem(x + d, nx)

    barrier = pltpu.get_barrier_semaphore()

    def greet(j, carry):
        pl.semaphore_signal(barrier, inc=1, device_id={"z": far_first(j)}, device_id_type=MESH)
        return carry

    lax.fori_loop(0, nz - 1, greet, 0)
    for d in range(1, ny):
        there = {"y": lax.rem(y + d, ny)}
        pl.semaphore_signal(barrier, inc=1, device_id=there, device_id_type=MESH)
    peers = [(dx, dc) for dx in range(nx) for dc in range(2)][1:]
    for dx, dc in peers:
        there = {"x": x_at(dx), "c": lax.rem(c + dc, 2)}
        pl.semaphore_signal(barrier, inc=1, device_id=there, device_id_type=MESH)

    for h in range(heads):
        onehot_t = (
            lax.broadcasted_iota(jnp.int32, (ncodes, tokens), 0) == row_ref[h : h + 1, :]
        ).astype(BF16)
        both = jnp.concatenate([v_ref[h], jnp.ones((tokens, width), BF16)], axis=1)
        summed = dot_nn(onehot_t, both)
        sums[h] = summed[:, :width].astype(BF16).reshape(nz, sl, width)
        lane = lax.broadcasted_iota(jnp.int32, (ncodes, width), 1)
        code = lax.broadcasted_iota(jnp.int32, (ncodes, width), 0)
        mine = jnp.where(lane == h * sl + lax.rem(code, sl), summed[:, width:], 0.0)
        counted = jnp.sum(mine.reshape(nz, sl, width), axis=1)
        if h == 0:
            counts = counted
        else:
            counts = counts + counted
    csums[...] = counts.reshape(nz, 1, width)

    def block_scores(h):
        onehot = (
            lax.broadcasted_iota(jnp.int32, (tokens, ncodes), 1) == col_ref[:, h : h + 1]
        ).astype(BF16)
        keys = dot_nn(onehot, book_ref[h]).astype(BF16)
        scale = width ** (-0.5)
        code_sc[h] = dot_nt(q_ref[h], book_ref[h]) * scale
        scores = dot_nt(q_ref[h], keys) * scale
        rows = lax.broadcasted_iota(jnp.int32, (tokens, tokens), 0)
        ends = lax.broadcasted_iota(jnp.int32, (tokens, tokens), 1)
        scores = jnp.where(rows >= ends, scores, NEG)
        top = jnp.max(scores, axis=1, keepdims=True)
        weights = jnp.exp(scores - top)
        aloc[h] = dot_nn(weights.astype(BF16), v_ref[h])
        stat[h, 0] = top
        stat[h, 1] = jnp.sum(weights, axis=1, keepdims=True)

    pl.semaphore_wait(barrier, nz - 1 + ny - 1 + len(peers))

    def z_push(source, target, chunk):
        def push(j, carry):
            there = far_first(j)
            pltpu.make_async_remote_copy(
                src_ref=source.at[there],
                dst_ref=target.at[z],
                send_sem=z_send.at[chunk],
                recv_sem=z_recv.at[chunk],
                device_id={"z": there},
                device_id_type=MESH,
            ).start()
            return carry

        lax.fori_loop(0, nz - 1, push, 0)
        target[z] = source[z]

    z_push(csums, craw, 0)
    for h in range(heads):
        z_push(sums.at[h], raw.at[h], 1 + h)

    def w_slice(dx, dc):
        owner = x_at(dx) * 2 + lax.rem(c + dc, 2)
        return w_ref.at[:, pl.ds(pl.multiple_of(owner * cols, cols), cols)]

    own_w = pltpu.make_async_copy(w_slice(0, 0), wcol.at[0, 0], w_local)
    own_w.start()
    w_copies = []
    for dx, dc in peers:
        copy = pltpu.make_async_remote_copy(
            src_ref=w_slice(dx, dc),
            dst_ref=wcol.at[(nx - dx) % nx, dc],
            send_sem=w_send.at[dx, dc],
            recv_sem=w_recv.at[(nx - dx) % nx, dc],
            device_id={"x": x_at(dx), "c": lax.rem(c + dc, 2)},
            device_id_type=MESH,
        )
        copy.start()
        w_copies.append(copy)

    for h in range(heads):
        block_scores(h)

    def scan_z(read, chunk, received, store_total, store):
        wait_bytes(received, z_recv.at[chunk])
        before = []
        so_far = None
        for n in range(nz):
            part = read(n)
            before.append(so_far)
            so_far = part if so_far is None else so_far + part
        store_total(so_far)
        for n in range(nz):
            store(n, jnp.zeros_like(so_far) if before[n] is None else before[n])

    def y_push(source, target, chunk):
        for d in range(1, ny):
            pltpu.make_async_remote_copy(
                src_ref=source,
                dst_ref=target.at[ny - d],
                send_sem=y_send.at[chunk],
                recv_sem=y_recv.at[chunk],
                device_id={"y": lax.rem(y + d, ny)},
                device_id_type=MESH,
            ).start()

    def earlier_rows(target, chunk):
        wait_bytes(target.at[pl.ds(1, ny - 1)], y_recv.at[chunk])
        total = None
        for d in range(1, ny):
            part = jnp.where(y + d >= ny, target[d].astype(F32), 0.0)
            total = part if total is None else total + part
        return total

    wait_bytes(craw.at[pl.ds(0, nz - 1)], z_recv.at[0])
    before, so_far = [], jnp.zeros((1, width), F32)
    for n in range(nz):
        before.append(so_far)
        so_far = so_far + craw[n]
    ctot_s[...] = so_far
    y_push(ctot_s, ctot_r, 0)
    above = earlier_rows(ctot_r, 0)
    for n in range(nz):
        cpre_s[n] = before[n] + above
    z_push(cpre_s, ccache, 3)

    def head_prefix(h):
        wait_bytes(raw.at[h, pl.ds(0, nz - 1)], z_recv.at[1 + h])
        before, so_far = [], jnp.zeros((sl, width), F32)
        for n in range(nz):
            before.append(so_far)
            so_far = so_far + raw[h, n].astype(F32)
        tot_s[h] = so_far.astype(BF16)
        y_push(tot_s.at[h], tot_r.at[h], 1 + h)
        above = earlier_rows(tot_r.at[h], 1 + h)
        for n in range(nz):
            pre_s[h, n] = (before[n] + above).astype(BF16)
        z_push(pre_s.at[h], cache.at[h], 4 + h)

    for h in range(heads):
        head_prefix(h)

    wait_bytes(ccache.at[pl.ds(0, nz - 1)], z_recv.at[3])
    found = ccache[...].reshape(nz, width)
    for h in range(heads):
        lane = lax.broadcasted_iota(jnp.int32, (width, ncodes), 0)
        code = lax.broadcasted_iota(jnp.int32, (width, ncodes), 1)
        pick = (lane == h * sl + lax.rem(code, sl)).astype(F32)
        spread = dot_nn(found, pick, lax.Precision.HIGHEST)
        group = lax.broadcasted_iota(jnp.int32, (nz, ncodes), 0)
        where = lax.broadcasted_iota(jnp.int32, (nz, ncodes), 1) // sl
        count = jnp.sum(jnp.where(group == where, spread, 0.0), axis=0, keepdims=True)
        scores = jnp.where(count > 0.0, code_sc[h], NEG)
        top = jnp.maximum(stat[h, 0], jnp.max(scores, axis=1, keepdims=True))
        weights = jnp.exp(scores - top)
        shift = jnp.exp(stat[h, 0] - top)
        den = stat[h, 1] * shift + jnp.sum(weights * count, axis=1, keepdims=True)
        inverse = 1.0 / den
        fw[h] = (weights * inverse).astype(BF16)
        aloc[h] = aloc[h] * (shift * inverse)

    def g_copy(h, r, slot, dx, dc, number):
        sx, sc = slot
        rows = pl.ds(r * half, half)
        return pltpu.make_async_remote_copy(
            src_ref=gath.at[h, sx, sc, rows],
            dst_ref=gath.at[h, (sx - dx) % nx, (sc + dc) % 2, rows],
            send_sem=g_send.at[h, number],
            recv_sem=g_recv.at[h, (sx - dx) % nx, (sc + dc) % 2, r],
            device_id={"x": x_at(dx), "c": lax.rem(c + dc, 2)},
            device_id_type=MESH,
        )

    right, left = 1, nx - 1
    sent = []

    def send(h, r, slot, dx, dc):
        number = sum(1 for other, _ in sent if other == h)
        copy = g_copy(h, r, slot, dx, dc, number)
        copy.start()
        sent.append((h, copy))

    def landed(h, r, slot):
        sx, sc = slot
        ref = gath.at[h, sx, sc, pl.ds(r * half, half)]
        wait_bytes(ref, g_recv.at[h, sx, sc, r])

    def finish(h):
        wait_bytes(cache.at[h, pl.ds(0, nz - 1)], z_recv.at[4 + h])
        table = cache[h].reshape(ncodes, width)
        gath[h, 0, 0] = (aloc[h] + dot_nn(fw[h], table)).astype(BF16)
        for r in range(2):
            send(h, r, (0, 0), right, 0)
            send(h, 1 - r, (0, 0), left, 0)
        for r in range(2):
            send(h, r, (0, 0), 0, 1)

    def relay(h):
        landed(h, 0, (left, 0))
        send(h, 0, (left, 0), right, 0)
        send(h, 0, (left, 0), 0, 1)
        landed(h, 1, (right, 0))
        send(h, 1, (right, 0), left, 0)
        send(h, 1, (right, 0), 0, 1)
        landed(h, 1, (left, 0))
        send(h, 1, (left, 0), 0, 1)
        landed(h, 0, (right, 0))
        send(h, 0, (right, 0), 0, 1)
        for r in range(2):
            landed(h, r, (2, 0))
            send(h, r, (2, 0), 0, 1)

    def project(h, slots, total):
        for sx, sc in slots:
            part = dot_nn(gath[h, sx, sc], wcol[sx, sc, h * width : (h + 1) * width, :])
            total = part if total is None else total + part
        return total

    direct = [(0, 0), (left, 0), (right, 0), (2, 0)]
    other = [(0, 1), (left, 1), (right, 1), (2, 1)]

    finish(0)
    relay(0)
    finish(1)
    own_w.wait()
    for copy in w_copies:
        copy.wait()
    relay(1)
    total = project(0, direct, None)
    for slot in other:
        for r in range(2):
            landed(0, r, slot)
    total = project(0, other, total)
    total = project(1, direct, total)
    for slot in other:
        for r in range(2):
            landed(1, r, slot)
    total = project(1, other, total)
    out_ref[...] = total.astype(BF16)

    for _, copy in sent:
        copy.wait_send()
    for chunk, ref in ((0, csums), (1, sums.at[0]), (2, sums.at[1])):
        wait_bytes(ref.at[pl.ds(0, nz - 1)], z_send.at[chunk])
    for chunk, ref in ((3, cpre_s), (4, pre_s.at[0]), (5, pre_s.at[1])):
        wait_bytes(ref.at[pl.ds(0, nz - 1)], z_send.at[chunk])
    for chunk, ref in ((0, ctot_r), (1, tot_r.at[0]), (2, tot_r.at[1])):
        wait_bytes(ref.at[pl.ds(1, ny - 1)], y_send.at[chunk])


def on_device(queries, values, codes, codebook, out_weight, *, ny, nz, nx):
    tokens, heads, width = queries.shape
    ncodes = codebook.shape[1]
    sl = ncodes // nz
    cols = out_weight.shape[1] // (nx * 2)
    depth = out_weight.shape[0]
    vmem = pl.BlockSpec(memory_space=pltpu.VMEM)
    scratch = [
        pltpu.VMEM((heads, nz, sl, width), BF16),
        pltpu.VMEM((heads, nz, sl, width), BF16),
        pltpu.VMEM((heads, sl, width), BF16),
        pltpu.VMEM((heads, ny, sl, width), BF16),
        pltpu.VMEM((heads, nz, sl, width), BF16),
        pltpu.VMEM((heads, nz, sl, width), BF16),
        pltpu.VMEM((nz, 1, width), F32),
        pltpu.VMEM((nz, 1, width), F32),
        pltpu.VMEM((1, width), F32),
        pltpu.VMEM((ny, 1, width), F32),
        pltpu.VMEM((nz, 1, width), F32),
        pltpu.VMEM((nz, 1, width), F32),
        pltpu.VMEM((heads, tokens, ncodes), F32),
        pltpu.VMEM((heads, tokens, ncodes), BF16),
        pltpu.VMEM((heads, tokens, width), F32),
        pltpu.VMEM((heads, 2, tokens, 1), F32),
        pltpu.VMEM((heads, nx, 2, tokens, width), BF16),
        pltpu.VMEM((nx, 2, depth, cols), BF16),
        pltpu.SemaphoreType.DMA((6,)),
        pltpu.SemaphoreType.DMA((6,)),
        pltpu.SemaphoreType.DMA((3,)),
        pltpu.SemaphoreType.DMA((3,)),
        pltpu.SemaphoreType.DMA((nx, 2)),
        pltpu.SemaphoreType.DMA((nx, 2)),
        pltpu.SemaphoreType.DMA,
        pltpu.SemaphoreType.DMA((heads, 16)),
        pltpu.SemaphoreType.DMA((heads, nx, 2, 2)),
    ]
    return pl.pallas_call(
        functools.partial(kernel, ny=ny, nz=nz, nx=nx),
        out_shape=jax.ShapeDtypeStruct((tokens, cols), BF16),
        in_specs=[vmem] * 5 + [pl.BlockSpec(memory_space=pl.ANY)],
        out_specs=vmem,
        scratch_shapes=scratch,
        compiler_params=pltpu.CompilerParams(collective_id=0, has_side_effects=True),
        name="vq_layer",
    )(
        jnp.swapaxes(queries, 0, 1),
        jnp.swapaxes(values, 0, 1),
        codes,
        codes.T,
        codebook,
        out_weight,
    )


def layer(mesh, ny, nz, nx):
    finer = Mesh(mesh.devices.reshape(ny, nz, nx, 2), ("y", "z", "x", "c"))
    placed = (
        P(CTX, HEAD, None),
        P(CTX, HEAD, None),
        P(CTX, HEAD),
        P(HEAD, None, None),
        P(HEAD, None),
    )
    return jax.shard_map(
        functools.partial(on_device, ny=ny, nz=nz, nx=nx),
        mesh=finer,
        in_specs=placed,
        out_specs=P(CTX, HEAD),
        check_vma=False,
    )


def solution(mesh):
    return layer(mesh, 4, 16, 4)
```

time: 176 us -> 67.2 us (0.38)
  blocking collectives: 67.9 us -> 0 us
  Pallas kernels: 0 us -> 61.7 us
  waiting for transfers between devices: 33.5 us -> 0 us
  starting transfers between devices: 22.3 us -> 0 us
  matrix products: 17.1 us -> 0 us
  between operations: 13.6 us -> 0.01 us
  local copies, waits for them, and re-layouts: 15 us -> 5.04 us
  other arithmetic: 6.21 us -> 0 us
    pallas_call x0 -> x1, Pallas kernels: none -> 61.7 us  [on_device(): pl.pallas_call(functools.partial(kernel, ny=ny, nz=nz, nx=nx), out_shape=...]
    all_gather x2 -> x0, blocking collectives: 34.9 us -> none  [prefix_by_axis(): lax.all_gather(part.astype(kind), axis)]
    all_gather x2 -> x0, waiting for transfers between devices: 33.5 us -> none  [prefix_by_axis(): lax.all_gather(part.astype(kind), axis)]
    all_to_all x1 -> x0, blocking collectives: 33 us -> none  [sent_to_all(): return lax.all_to_all(copies, axis, split_axis=0, concat_axis=0, tiled=True)]
    dot_general x8 -> x0, matrix products: 17.1 us -> none  [the longest x1 5.19 us: attend(): jnp.dot(code_weight, cache_sum, precision=lax.Precision.HIGHEST)]
    ppermute x4 -> x0, starting transfers between devices: 16.2 us -> none  [from_behind(): lax.ppermute(value, axis, [(source, source + steps) for source in range(f...]
    gather x1 -> x0, local copies, waits for them, and re-layouts: 10.5 us -> none  [on_device(): book[index]]
    all_to_all x1 -> x0, starting transfers between devices: 6.09 us -> none  [on_device(): lax.all_to_all(out_weight, 'head', split_axis=1, concat_axis=0, tiled=True)]
  transfers between devices with their start and end apart: 7 -> 0, of which waited for: 2 -> 0; matrix products, arithmetic and copies ran while one was open for 18% -> 0% of each run, Pallas kernels for 0% -> 0%
where the time goes in v1:
time: 67.2 us; the launch traced here: 66.7 us
  Pallas kernels  61.7 us (92%)
  local copies, waits for them, and re-layouts  5.04 us (8%)
    pallas_call x1, Pallas kernels, on_device(): pl.pallas_call(functools.partial(kernel, ny=ny, nz=nz, nx=nx), out_shape=...  61.7 us
    unnamed x4, local copies, waits for them, and re-layouts  3.24 us
    transpose x1, local copies, waits for them, and re-layouts, on_device(): jnp.swapaxes(values, 0, 1)  1.79 us

profile of v1, /device:TPU:1, one launch (start us, length us, event | category | flops | bytes accessed | tf_op | source)
XLA Modules:
  0.0 66.7 jit_solution(14714155178283204378)
XLA Ops:
  0.0 0.0 copy-start
  0.0 1.6 %copy.8.col_ref = s32[512,2]{1,0:T(8,128)} copy(s32[512,2]{0,1:T(2,128)} %param.7) | data formatting | bytes 8192 | tf_op args[2]
  1.6 0.0 copy-done
  1.6 1.8 %copy_bitcast_fusion = (bf16[2,512,128]{2,1,0:T(8,128)(2,1)}, bf16[2,512,128]{2,1,0:T(8,128)(2,1)}) fusion(bf16[512,2,128]{2,1,0:T(2,128)(2,1)S(1)} %copy-done, bf16[512,2,128]{2,1,0:T(2,128)(2,1)} %param.5), kind=kLoop, calls=%fused_computation | loop fusion | bytes 1048576 | tf_op jit(solution)/shard_map/transpose | solution.py:362
  3.4 61.7 %vq_layer.1 = bf16[512,256]{1,0:T(8,128)(2,1)} custom-call(bf16[2,512,128]{2,1,0:T(8,128)(2,1)} %get-tuple-element.6.q_ref, bf16[2,512,128]{2,1,0:T(8,128)(2,1)} %get-tuple-element.5.v_ref, s32[512,2]{1,0:T(8,128)} %copy.8.col_ref, s32[2,512]{1,0:T(2,128)} %bitcast.5, bf16[2,512,128]{2,1,0:T(8,128)(2,1)} %book_ref.1, bf16[256,2048]{1,0:T(8,128)(2,1)} %w_ref.1), custom_call_target="tpu_custom_call" | custom-call | tf_op jit(solution)/shard_map/vq_layer/pallas_call | solution.py:352
  65.1 1.7 %copy.12 = bf16[512,256]{1,0:T(8,128)(2,1)} copy(bf16[512,256]{1,0:T(8,128)(2,1)} %vq_layer.1) | data formatting | bytes 524288
Async XLA Ops:
  0.0 1.6 %copy-start = (bf16[512,2,128]{2,1,0:T(2,128)(2,1)S(1)}, bf16[512,2,128]{2,1,0:T(2,128)(2,1)}, u32[]{:S(2)}) copy-start(bf16[512,2,128]{2,1,0:T(2,128)(2,1)} %param.6) | copy-start | bytes 786436

commit v2 on v1

v2 whole, which is shorter than its diff:
```python
import functools

import jax
import jax.numpy as jnp
from jax import lax
from jax.experimental import pallas as pl
from jax.experimental.pallas import tpu as pltpu
from jax.sharding import Mesh
from jax.sharding import PartitionSpec as P

MESH = pl.DeviceIdType.MESH
CTX = ("y", "z")
HEAD = ("x", "c")
F32 = jnp.float32
BF16 = jnp.bfloat16
NEG = float("-inf")


def dot_nt(a, b):
    return lax.dot_general(a, b, (((1,), (1,)), ((), ())), preferred_element_type=F32)


def dot_nn(a, b, precision=None):
    return lax.dot_general(
        a, b, (((1,), (0,)), ((), ())), precision=precision, preferred_element_type=F32
    )


def dot_tn(a, b):
    return lax.dot_general(a, b, (((0,), (0,)), ((), ())), preferred_element_type=F32)


def wait_bytes(ref, sem):
    pltpu.make_async_copy(ref, ref, sem).wait()


def kernel(
    q_ref, v_ref, row_ref, book_ref, w_ref, out_ref,
    qin, vin, codes, book, split, vals, qs,
    sums, raw, tot_s, tot_r, pre_s, cache,
    csums, craw, ctot_s, ctot_r, cpre_s, ccache,
    code_sc, fw, aloc, stat, gath, wcol, acc,
    in_sem, z_send, z_recv, y_send, y_recv, w_send, w_recv, w_local, g_send, g_recv,
    *, ny, nz, nx, nch,
):
    heads, ncodes, width = book_ref.shape
    tokens = q_ref.shape[0] // heads
    sl = ncodes // nz
    part = tokens // nch
    cols = out_ref.shape[1]
    y, z, x, c = (lax.axis_index(name) for name in ("y", "z", "x", "c"))
    scope = jax.named_scope

    def far_first(j):
        step = (j + 1) // 2
        sign = 1 - 2 * lax.rem(j, 2)
        return lax.rem(z + nz // 2 + sign * step + nz, nz)

    def x_at(d):
        return lax.rem(x + d, nx)

    barrier = pltpu.get_barrier_semaphore()

    def greet(j, carry):
        pl.semaphore_signal(barrier, inc=1, device_id={"z": far_first(j)}, device_id_type=MESH)
        return carry

    lax.fori_loop(0, nz - 1, greet, 0)
    for d in range(1, ny):
        there = {"y": lax.rem(y + d, ny)}
        pl.semaphore_signal(barrier, inc=1, device_id=there, device_id_type=MESH)
    peers = [(dx, dc) for dx in range(nx) for dc in range(2)][1:]
    for dx, dc in peers:
        there = {"x": x_at(dx), "c": lax.rem(c + dc, 2)}
        pl.semaphore_signal(barrier, inc=1, device_id=there, device_id_type=MESH)

    loads = []
    for number, (source, target) in enumerate(
        ((row_ref, codes), (v_ref, vin), (book_ref, book), (q_ref, qin))
    ):
        loads.append(pltpu.make_async_copy(source, target, in_sem.at[number]))
        loads[-1].start()

    with scope("load"):
        loads[0].wait()
        loads[1].wait()
    with scope("sums"):
        split[...] = vin[...].astype(F32)
        counts = None
        for h in range(heads):
            vals[h] = split[pl.ds(h, tokens, stride=heads), :].astype(BF16)
            onehot_t = (
                lax.broadcasted_iota(jnp.int32, (ncodes, tokens), 0) == codes[h : h + 1, :]
            ).astype(BF16)
            both = jnp.concatenate([vals[h], jnp.ones((tokens, width), BF16)], axis=1)
            summed = dot_nn(onehot_t, both)
            sums[h] = summed[:, :width].astype(BF16).reshape(nz, sl, width)
            lane = lax.broadcasted_iota(jnp.int32, (ncodes, width), 1)
            code = lax.broadcasted_iota(jnp.int32, (ncodes, width), 0)
            mine = jnp.where(lane == h * sl + lax.rem(code, sl), summed[:, width:], 0.0)
            counted = jnp.sum(mine.reshape(nz, sl, width), axis=1)
            counts = counted if counts is None else counts + counted
        csums[...] = counts.reshape(nz, 1, width)

    def block_scores(h):
        onehot_t = (
            lax.broadcasted_iota(jnp.int32, (ncodes, tokens), 0) == codes[h : h + 1, :]
        ).astype(BF16)
        keys_t = dot_tn(book[h], onehot_t).astype(BF16)
        scale = width ** (-0.5)
        code_sc[h] = dot_nt(qs[h], book[h]) * scale
        scores = dot_nn(qs[h], keys_t) * scale
        rows = lax.broadcasted_iota(jnp.int32, (tokens, tokens), 0)
        ends = lax.broadcasted_iota(jnp.int32, (tokens, tokens), 1)
        scores = jnp.where(rows >= ends, scores, NEG)
        top = jnp.max(scores, axis=1, keepdims=True)
        weights = jnp.exp(scores - top)
        aloc[h] = dot_nn(weights.astype(BF16), vals[h])
        stat[h, 0] = top
        stat[h, 1] = jnp.sum(weights, axis=1, keepdims=True)

    with scope("barrier"):
        pl.semaphore_wait(barrier, nz - 1 + ny - 1 + len(peers))

    def z_push(source, target, chunk):
        def push(j, carry):
            there = far_first(j)
            pltpu.make_async_remote_copy(
                src_ref=source.at[there],
                dst_ref=target.at[z],
                send_sem=z_send.at[chunk],
                recv_sem=z_recv.at[chunk],
                device_id={"z": there},
                device_id_type=MESH,
            ).start()
            return carry

        lax.fori_loop(0, nz - 1, push, 0)
        target[z] = source[z]

    with scope("push_raw"):
        z_push(csums, craw, 0)
        for h in range(heads):
            z_push(sums.at[h], raw.at[h], 1 + h)

    def w_slice(dx, dc):
        owner = x_at(dx) * 2 + lax.rem(c + dc, 2)
        return w_ref.at[:, pl.ds(pl.multiple_of(owner * cols, cols), cols)]

    own_w = pltpu.make_async_copy(w_slice(0, 0), wcol.at[0, 0], w_local)
    own_w.start()
    w_copies = []
    for dx, dc in peers:
        copy = pltpu.make_async_remote_copy(
            src_ref=w_slice(dx, dc),
            dst_ref=wcol.at[(nx - dx) % nx, dc],
            send_sem=w_send.at[dx, dc],
            recv_sem=w_recv.at[(nx - dx) % nx, dc],
            device_id={"x": x_at(dx), "c": lax.rem(c + dc, 2)},
            device_id_type=MESH,
        )
        copy.start()
        w_copies.append(copy)

    with scope("scores"):
        loads[2].wait()
        loads[3].wait()
        split[...] = qin[...].astype(F32)
        for h in range(heads):
            qs[h] = split[pl.ds(h, tokens, stride=heads), :].astype(BF16)
            block_scores(h)

    def y_push(source, target, chunk):
        for d in range(1, ny):
            pltpu.make_async_remote_copy(
                src_ref=source,
                dst_ref=target.at[ny - d],
                send_sem=y_send.at[chunk],
                recv_sem=y_recv.at[chunk],
                device_id={"y": lax.rem(y + d, ny)},
                device_id_type=MESH,
            ).start()

    with scope("wait_craw"):
        wait_bytes(craw.at[pl.ds(0, nz - 1)], z_recv.at[0])
    cbefore, so_far = [], jnp.zeros((1, width), F32)
    for n in range(nz):
        cbefore.append(so_far)
        so_far = so_far + craw[n]
    ctot_s[...] = so_far
    y_push(ctot_s, ctot_r, 0)
    for h in range(heads):
        with scope(f"wait_raw{h}"):
            wait_bytes(raw.at[h, pl.ds(0, nz - 1)], z_recv.at[1 + h])
        so_far = raw[h, 0].astype(F32)
        for n in range(1, nz):
            so_far = so_far + raw[h, n].astype(F32)
        tot_s[h] = so_far.astype(BF16)
    y_push(tot_s, tot_r, 1)

    def earlier_rows(target):
        total = None
        for d in range(1, ny):
            row = jnp.where(y + d >= ny, target(d).astype(F32), 0.0)
            total = row if total is None else total + row
        return total

    with scope("wait_cy"):
        wait_bytes(ctot_r.at[pl.ds(1, ny - 1)], y_recv.at[0])
    above = earlier_rows(lambda d: ctot_r[d])
    for n in range(nz):
        cpre_s[n] = cbefore[n] + above
    z_push(cpre_s, ccache, 3)
    with scope("wait_y"):
        wait_bytes(tot_r.at[pl.ds(1, ny - 1)], y_recv.at[1])
    with scope("prefix"):
        for h in range(heads):
            so_far = earlier_rows(lambda d, h=h: tot_r[d, h])
            for n in range(nz):
                pre_s[h, n] = so_far.astype(BF16)
                so_far = so_far + raw[h, n].astype(F32)
            z_push(pre_s.at[h], cache.at[h], 4 + h)

    with scope("wait_ccache"):
        wait_bytes(ccache.at[pl.ds(0, nz - 1)], z_recv.at[3])

    def code_weights(h):
        lane = lax.broadcasted_iota(jnp.int32, (width, ncodes), 0)
        code = lax.broadcasted_iota(jnp.int32, (width, ncodes), 1)
        pick = (lane == h * sl + lax.rem(code, sl)).astype(F32)
        spread = dot_nn(found, pick, lax.Precision.HIGHEST)
        group = lax.broadcasted_iota(jnp.int32, (nz, ncodes), 0)
        where = lax.broadcasted_iota(jnp.int32, (nz, ncodes), 1) // sl
        count = jnp.sum(jnp.where(group == where, spread, 0.0), axis=0, keepdims=True)
        scores = jnp.where(count > 0.0, code_sc[h], NEG)
        top = jnp.maximum(stat[h, 0], jnp.max(scores, axis=1, keepdims=True))
        weights = jnp.exp(scores - top)
        shift = jnp.exp(stat[h, 0] - top)
        den = stat[h, 1] * shift + jnp.sum(weights * count, axis=1, keepdims=True)
        inverse = 1.0 / den
        fw[h] = (weights * inverse).astype(BF16)
        aloc[h] = aloc[h] * (shift * inverse)

    with scope("weights"):
        found = ccache[...].reshape(nz, width)
        for h in range(heads):
            code_weights(h)

    right, left = 1, nx - 1

    def piece(slot, h, r):
        return gath.at[slot[0], slot[1], pl.ds(r * part, part), pl.ds(h * width, width)]

    copies = []

    def send(h, r, slot, dx, dc):
        there = ((slot[0] - dx) % nx, (slot[1] + dc) % 2)
        copy = pltpu.make_async_remote_copy(
            src_ref=piece(slot, h, r),
            dst_ref=piece(there, h, r),
            send_sem=g_send.at[len(copies)],
            recv_sem=g_recv.at[h, there[0], there[1], r],
            device_id={"x": x_at(dx), "c": lax.rem(c + dc, 2)},
            device_id_type=MESH,
        )
        copy.start()
        copies.append(copy)

    def landed(h, r, slot):
        wait_bytes(piece(slot, h, r), g_recv.at[h, slot[0], slot[1], r])

    low, high = range(nch // 2), range(nch // 2, nch)
    for h in range(heads):
        with scope(f"wait_cache{h}"):
            wait_bytes(cache.at[h, pl.ds(0, nz - 1)], z_recv.at[4 + h])
        table = cache[h].reshape(ncodes, width)
        gath[0, 0, :, h * width : (h + 1) * width] = (aloc[h] + dot_nn(fw[h], table)).astype(BF16)
        for r, s in zip((*low, *high), (*high, *low), strict=True):
            send(h, r, (0, 0), right, 0)
            send(h, s, (0, 0), left, 0)
        for r in range(nch):
            send(h, r, (0, 0), 0, 1)

    def project(slot, first=False):
        add = dot_nn(gath[slot[0], slot[1]], wcol[slot[0], slot[1]])
        acc[...] = add if first else acc[...] + add

    with scope("wait_w"):
        own_w.wait()
        for copy in w_copies:
            copy.wait()
    project((0, 0), True)
    for h in range(heads):
        with scope(f"relay{h}"):
            for r, s in zip(low, high, strict=True):
                landed(h, r, (left, 0))
                send(h, r, (left, 0), right, 0)
                send(h, r, (left, 0), 0, 1)
                landed(h, s, (right, 0))
                send(h, s, (right, 0), left, 0)
                send(h, s, (right, 0), 0, 1)
            for r, s in zip(high, low, strict=True):
                landed(h, r, (left, 0))
                send(h, r, (left, 0), 0, 1)
                landed(h, s, (right, 0))
                send(h, s, (right, 0), 0, 1)
    for h in range(heads):
        with scope(f"across{h}"):
            for r, s in zip(low, high, strict=True):
                landed(h, r, (2, 0))
                send(h, r, (2, 0), 0, 1)
                landed(h, s, (2, 0))
                send(h, s, (2, 0), 0, 1)
    for slot in ((left, 0), (right, 0), (2, 0)):
        project(slot)
    for slot in ((0, 1), (left, 1), (right, 1), (2, 1)):
        with scope("other"):
            for h in range(heads):
                for r in range(nch):
                    landed(h, r, slot)
        project(slot)
    out_ref[...] = acc[...].astype(BF16)

    with scope("tail"):
        for copy in copies:
            copy.wait_send()
        for chunk, ref in ((0, csums), (1, sums.at[0]), (2, sums.at[1])):
            wait_bytes(ref.at[pl.ds(0, nz - 1)], z_send.at[chunk])
        for chunk, ref in ((3, cpre_s), (4, pre_s.at[0]), (5, pre_s.at[1])):
            wait_bytes(ref.at[pl.ds(0, nz - 1)], z_send.at[chunk])
        for chunk, ref in ((0, ctot_r), (1, tot_r)):
            wait_bytes(ref.at[pl.ds(1, ny - 1)], y_send.at[chunk])


def on_device(queries, values, codes, codebook, out_weight, *, ny, nz, nx):
    tokens, heads, width = queries.shape
    ncodes = codebook.shape[1]
    sl = ncodes // nz
    cols = out_weight.shape[1] // (nx * 2)
    depth = out_weight.shape[0]
    nch = 4
    anywhere = pl.BlockSpec(memory_space=pl.ANY)
    ncopies = heads * (3 * nch + nch + 3 * nch)
    scratch = [
        pltpu.VMEM((tokens * heads, width), BF16),
        pltpu.VMEM((tokens * heads, width), BF16),
        pltpu.VMEM((heads, tokens), jnp.int32),
        pltpu.VMEM((heads, ncodes, width), BF16),
        pltpu.VMEM((tokens * heads, width), F32),
        pltpu.VMEM((heads, tokens, width), BF16),
        pltpu.VMEM((heads, tokens, width), BF16),
        pltpu.VMEM((heads, nz, sl, width), BF16),
        pltpu.VMEM((heads, nz, sl, width), BF16),
        pltpu.VMEM((heads, sl, width), BF16),
        pltpu.VMEM((ny, heads, sl, width), BF16),
        pltpu.VMEM((heads, nz, sl, width), BF16),
        pltpu.VMEM((heads, nz, sl, width), BF16),
        pltpu.VMEM((nz, 1, width), F32),
        pltpu.VMEM((nz, 1, width), F32),
        pltpu.VMEM((1, width), F32),
        pltpu.VMEM((ny, 1, width), F32),
        pltpu.VMEM((nz, 1, width), F32),
        pltpu.VMEM((nz, 1, width), F32),
        pltpu.VMEM((heads, tokens, ncodes), F32),
        pltpu.VMEM((heads, tokens, ncodes), BF16),
        pltpu.VMEM((heads, tokens, width), F32),
        pltpu.VMEM((heads, 2, tokens, 1), F32),
        pltpu.VMEM((nx, 2, tokens, depth), BF16),
        pltpu.VMEM((nx, 2, depth, cols), BF16),
        pltpu.VMEM((tokens, cols), F32),
        pltpu.SemaphoreType.DMA((4,)),
        pltpu.SemaphoreType.DMA((6,)),
        pltpu.SemaphoreType.DMA((6,)),
        pltpu.SemaphoreType.DMA((2,)),
        pltpu.SemaphoreType.DMA((2,)),
        pltpu.SemaphoreType.DMA((nx, 2)),
        pltpu.SemaphoreType.DMA((nx, 2)),
        pltpu.SemaphoreType.DMA,
        pltpu.SemaphoreType.DMA((ncopies,)),
        pltpu.SemaphoreType.DMA((heads, nx, 2, nch)),
    ]
    return pl.pallas_call(
        functools.partial(kernel, ny=ny, nz=nz, nx=nx, nch=nch),
        out_shape=pltpu.VMEM((tokens, cols), BF16),
        in_specs=[anywhere] * 5,
        out_specs=pl.BlockSpec(memory_space=pltpu.VMEM),
        scratch_shapes=scratch,
        compiler_params=pltpu.CompilerParams(collective_id=0, has_side_effects=True),
        name="vq_layer",
    )(
        queries.reshape(tokens * heads, width),
        values.reshape(tokens * heads, width),
        codes.T,
        codebook,
        out_weight,
    )


def layer(mesh, ny, nz, nx):
    finer = Mesh(mesh.devices.reshape(ny, nz, nx, 2), ("y", "z", "x", "c"))
    placed = (
        P(CTX, HEAD, None),
        P(CTX, HEAD, None),
        P(CTX, HEAD),
        P(HEAD, None, None),
        P(HEAD, None),
    )
    return jax.shard_map(
        functools.partial(on_device, ny=ny, nz=nz, nx=nx),
        mesh=finer,
        in_specs=placed,
        out_specs=P(CTX, HEAD),
        check_vma=False,
    )


def solution(mesh):
    return layer(mesh, 4, 16, 4)
```

time: 67.2 us -> 59.6 us (0.89)
  local copies, waits for them, and re-layouts: 5.04 us -> 0.71 us
  Pallas kernels: 61.7 us -> 58.8 us
    pallas_call x1, Pallas kernels: 61.7 us -> 58.8 us  [on_device(): pl.pallas_call(functools.partial(kernel, ny=ny, nz=nz, nx=nx, nch=nch), o...]
    unnamed x4 -> x1, local copies, waits for them, and re-layouts: 3.24 us -> 0.71 us
    transpose x1 -> x0, local copies, waits for them, and re-layouts: 1.79 us -> none  [on_device(): jnp.swapaxes(values, 0, 1)]
where the time goes in v2:
time: 59.6 us; the launch traced here: 59.5 us
  Pallas kernels  58.8 us (99%)
  local copies, waits for them, and re-layouts  0.71 us (1%)
    pallas_call x1, Pallas kernels, on_device(): pl.pallas_call(functools.partial(kernel, ny=ny, nz=nz, nx=nx, nch=nch), o...  58.8 us

profile of v2, /device:TPU:1, one launch (start us, length us, event | category | flops | bytes accessed | tf_op | source)
XLA Modules:
  0.0 59.5 jit_solution(15635088655712173705)
XLA Ops:
  0.0 58.8 %vq_layer.1 = bf16[512,256]{1,0:T(8,128)(2,1)S(1)} custom-call(bf16[1024,128]{1,0:T(8,128)(2,1)} %bitcast.3, bf16[1024,128]{1,0:T(8,128)(2,1)} %bitcast.4, s32[2,512]{1,0:T(2,128)} %bitcast.5, bf16[2,512,128]{2,1,0:T(8,128)(2,1)} %book_ref.1, bf16[256,2048]{1,0:T(8,128)(2,1)} %w_ref.1), custom_call_target="tpu_custom_call" | custom-call | tf_op jit(solution)/shard_map/vq_layer/pallas_call | solution.py:382
  58.8 0.7 %copy.7 = bf16[512,256]{1,0:T(8,128)(2,1)} copy(bf16[512,256]{1,0:T(8,128)(2,1)S(1)} %vq_layer.1) | data formatting | bytes 524288

commit v3 on v2

--- a/solution.py
+++ b/solution.py
@@ -40,7 +40,7 @@
     sums, raw, tot_s, tot_r, pre_s, cache,
     csums, craw, ctot_s, ctot_r, cpre_s, ccache,
     code_sc, fw, aloc, stat, gath, wcol, acc,
-    in_sem, z_send, z_recv, y_send, y_recv, w_send, w_recv, w_local, g_send, g_recv,
+    in_sem, z_send, z_recv, y_send, y_recv, w_send, w_recv, w_local, g_send, g_recv, g_other,
     *, ny, nz, nx, nch,
 ):
     heads, ncodes, width = book_ref.shape
@@ -138,6 +138,25 @@
         lax.fori_loop(0, nz - 1, push, 0)
         target[z] = source[z]
 
+    def z_push_band(source, target, chunk, start, count):
+        def push(j, carry):
+            there = start + lax.rem(z + j, count)
+
+            @pl.when(there != z)
+            def _():
+                pltpu.make_async_remote_copy(
+                    src_ref=source.at[there],
+                    dst_ref=target.at[z],
+                    send_sem=z_send.at[chunk],
+                    recv_sem=z_recv.at[chunk],
+                    device_id={"z": there},
+                    device_id_type=MESH,
+                ).start()
+
+            return carry
+
+        lax.fori_loop(0, count, push, 0)
+
     with scope("push_raw"):
         z_push(csums, craw, 0)
         for h in range(heads):
@@ -147,20 +166,17 @@
         owner = x_at(dx) * 2 + lax.rem(c + dc, 2)
         return w_ref.at[:, pl.ds(pl.multiple_of(owner * cols, cols), cols)]
 
-    own_w = pltpu.make_async_copy(w_slice(0, 0), wcol.at[0, 0], w_local)
+    own_w = pltpu.make_async_copy(w_slice(0, 0), wcol.at[0], w_local)
     own_w.start()
-    w_copies = []
     for dx, dc in peers:
-        copy = pltpu.make_async_remote_copy(
+        pltpu.make_async_remote_copy(
             src_ref=w_slice(dx, dc),
-            dst_ref=wcol.at[(nx - dx) % nx, dc],
-            send_sem=w_send.at[dx, dc],
-            recv_sem=w_recv.at[(nx - dx) % nx, dc],
+            dst_ref=wcol.at[(nx - dx) % nx * 2 + dc],
+            send_sem=w_send,
+            recv_sem=w_recv,
             device_id={"x": x_at(dx), "c": lax.rem(c + dc, 2)},
             device_id_type=MESH,
-        )
-        copy.start()
-        w_copies.append(copy)
+        ).start()
 
     with scope("scores"):
         loads[2].wait()
@@ -189,37 +205,47 @@
         so_far = so_far + craw[n]
     ctot_s[...] = so_far
     y_push(ctot_s, ctot_r, 0)
-    for h in range(heads):
+    def row_total(h):
         with scope(f"wait_raw{h}"):
             wait_bytes(raw.at[h, pl.ds(0, nz - 1)], z_recv.at[1 + h])
         so_far = raw[h, 0].astype(F32)
         for n in range(1, nz):
             so_far = so_far + raw[h, n].astype(F32)
         tot_s[h] = so_far.astype(BF16)
-    y_push(tot_s, tot_r, 1)
+        y_push(tot_s.at[h], tot_r.at[h], 1 + h)
 
     def earlier_rows(target):
         total = None
         for d in range(1, ny):
-            row = jnp.where(y + d >= ny, target(d).astype(F32), 0.0)
+            row = jnp.where(y + d >= ny, target[d].astype(F32), 0.0)
             total = row if total is None else total + row
         return total
 
+    def send_prefix(h):
+        with scope(f"wait_y{h}"):
+            wait_bytes(tot_r.at[h, pl.ds(1, ny - 1)], y_recv.at[1 + h])
+        with scope(f"prefix{h}"):
+            so_far = earlier_rows(tot_r.at[h])
+            for n in range(nz):
+                pre_s[h, n] = so_far.astype(BF16)
+                so_far = so_far + raw[h, n].astype(F32)
+            cache[h, z] = pre_s[h, z]
+            z_push_band(pre_s.at[h], cache.at[h], 4 + h, 0, nz // 4)
+            z_push_band(pre_s.at[h], cache.at[h], 4 + h, nz // 4, nz // 4)
+
+    row_total(0)
     with scope("wait_cy"):
         wait_bytes(ctot_r.at[pl.ds(1, ny - 1)], y_recv.at[0])
-    above = earlier_rows(lambda d: ctot_r[d])
+    above = earlier_rows(ctot_r)
     for n in range(nz):
         cpre_s[n] = cbefore[n] + above
     z_push(cpre_s, ccache, 3)
-    with scope("wait_y"):
-        wait_bytes(tot_r.at[pl.ds(1, ny - 1)], y_recv.at[1])
-    with scope("prefix"):
-        for h in range(heads):
-            so_far = earlier_rows(lambda d, h=h: tot_r[d, h])
-            for n in range(nz):
-                pre_s[h, n] = so_far.astype(BF16)
-                so_far = so_far + raw[h, n].astype(F32)
-            z_push(pre_s.at[h], cache.at[h], 4 + h)
+    for h in range(1, heads):
+        row_total(h)
+    for h in range(heads):
+        send_prefix(h)
+    for h in range(heads):
+        z_push_band(pre_s.at[h], cache.at[h], 4 + h, nz // 2, nz // 2)
 
     with scope("wait_ccache"):
         wait_bytes(ccache.at[pl.ds(0, nz - 1)], z_recv.at[3])
@@ -251,26 +277,25 @@
     def piece(slot, h, r):
         return gath.at[slot[0], slot[1], pl.ds(r * part, part), pl.ds(h * width, width)]
 
-    copies = []
+    def arrival(h, r, slot):
+        return g_other.at[slot[0]] if slot[1] else g_recv.at[h, slot[0] - 1, r]
 
     def send(h, r, slot, dx, dc):
         there = ((slot[0] - dx) % nx, (slot[1] + dc) % 2)
-        copy = pltpu.make_async_remote_copy(
+        pltpu.make_async_remote_copy(
             src_ref=piece(slot, h, r),
             dst_ref=piece(there, h, r),
-            send_sem=g_send.at[len(copies)],
-            recv_sem=g_recv.at[h, there[0], there[1], r],
+            send_sem=g_send.at[1 if dc else 0],
+            recv_sem=arrival(h, r, there),
             device_id={"x": x_at(dx), "c": lax.rem(c + dc, 2)},
             device_id_type=MESH,
-        )
-        copy.start()
-        copies.append(copy)
+        ).start()
 
     def landed(h, r, slot):
-        wait_bytes(piece(slot, h, r), g_recv.at[h, slot[0], slot[1], r])
+        wait_bytes(piece(slot, h, r), arrival(h, r, slot))
 
     low, high = range(nch // 2), range(nch // 2, nch)
-    for h in range(heads):
+    def finish(h):
         with scope(f"wait_cache{h}"):
             wait_bytes(cache.at[h, pl.ds(0, nz - 1)], z_recv.at[4 + h])
         table = cache[h].reshape(ncodes, width)
@@ -281,16 +306,7 @@
         for r in range(nch):
             send(h, r, (0, 0), 0, 1)
 
-    def project(slot, first=False):
-        add = dot_nn(gath[slot[0], slot[1]], wcol[slot[0], slot[1]])
-        acc[...] = add if first else acc[...] + add
-
-    with scope("wait_w"):
-        own_w.wait()
-        for copy in w_copies:
-            copy.wait()
-    project((0, 0), True)
-    for h in range(heads):
+    def relay(h):
         with scope(f"relay{h}"):
             for r, s in zip(low, high, strict=True):
                 landed(h, r, (left, 0))
@@ -304,31 +320,48 @@
                 send(h, r, (left, 0), 0, 1)
                 landed(h, s, (right, 0))
                 send(h, s, (right, 0), 0, 1)
-    for h in range(heads):
+
+    def across(h):
         with scope(f"across{h}"):
             for r, s in zip(low, high, strict=True):
                 landed(h, r, (2, 0))
                 send(h, r, (2, 0), 0, 1)
                 landed(h, s, (2, 0))
                 send(h, s, (2, 0), 0, 1)
-    for slot in ((left, 0), (right, 0), (2, 0)):
+
+    def project(slot, first=False):
+        add = dot_nn(gath[slot[0], slot[1]], wcol[slot[0] * 2 + slot[1]])
+        acc[...] = add if first else acc[...] + add
+
+    finish(0)
+    finish(1)
+    with scope("wait_w"):
+        own_w.wait()
+        w_all = wcol.at[pl.ds(1, len(peers))]
+        wait_bytes(w_all, w_recv)
+        wait_bytes(w_all, w_send)
+    project((0, 0), True)
+    relay(0)
+    relay(1)
+    for slot in ((left, 0), (right, 0)):
         project(slot)
-    for slot in ((0, 1), (left, 1), (right, 1), (2, 1)):
-        with scope("other"):
-            for h in range(heads):
-                for r in range(nch):
-                    landed(h, r, slot)
+    across(0)
+    across(1)
+    for slot in ((2, 0), (0, 1), (left, 1), (right, 1), (2, 1)):
+        if slot[1]:
+            with scope("other"):
+                wait_bytes(gath.at[slot[0], slot[1]], g_other.at[slot[0]])
         project(slot)
     out_ref[...] = acc[...].astype(BF16)
 
     with scope("tail"):
-        for copy in copies:
-            copy.wait_send()
+        wait_bytes(gath.at[pl.ds(0, 3), 0], g_send.at[0])
+        wait_bytes(gath.at[pl.ds(0, nx), 0], g_send.at[1])
         for chunk, ref in ((0, csums), (1, sums.at[0]), (2, sums.at[1])):
             wait_bytes(ref.at[pl.ds(0, nz - 1)], z_send.at[chunk])
         for chunk, ref in ((3, cpre_s), (4, pre_s.at[0]), (5, pre_s.at[1])):
             wait_bytes(ref.at[pl.ds(0, nz - 1)], z_send.at[chunk])
-        for chunk, ref in ((0, ctot_r), (1, tot_r)):
+        for chunk, ref in ((0, ctot_r), (1, tot_r.at[0]), (2, tot_r.at[1])):
             wait_bytes(ref.at[pl.ds(1, ny - 1)], y_send.at[chunk])
 
 
@@ -340,7 +373,6 @@
     depth = out_weight.shape[0]
     nch = 4
     anywhere = pl.BlockSpec(memory_space=pl.ANY)
-    ncopies = heads * (3 * nch + nch + 3 * nch)
     scratch = [
         pltpu.VMEM((tokens * heads, width), BF16),
         pltpu.VMEM((tokens * heads, width), BF16),
@@ -352,7 +384,7 @@
         pltpu.VMEM((heads, nz, sl, width), BF16),
         pltpu.VMEM((heads, nz, sl, width), BF16),
         pltpu.VMEM((heads, sl, width), BF16),
-        pltpu.VMEM((ny, heads, sl, width), BF16),
+        pltpu.VMEM((heads, ny, sl, width), BF16),
         pltpu.VMEM((heads, nz, sl, width), BF16),
         pltpu.VMEM((heads, nz, sl, width), BF16),
         pltpu.VMEM((nz, 1, width), F32),
@@ -366,18 +398,19 @@
         pltpu.VMEM((heads, tokens, width), F32),
         pltpu.VMEM((heads, 2, tokens, 1), F32),
         pltpu.VMEM((nx, 2, tokens, depth), BF16),
-        pltpu.VMEM((nx, 2, depth, cols), BF16),
+        pltpu.VMEM((nx * 2, depth, cols), BF16),
         pltpu.VMEM((tokens, cols), F32),
         pltpu.SemaphoreType.DMA((4,)),
         pltpu.SemaphoreType.DMA((6,)),
         pltpu.SemaphoreType.DMA((6,)),
+        pltpu.SemaphoreType.DMA((3,)),
+        pltpu.SemaphoreType.DMA((3,)),
+        pltpu.SemaphoreType.DMA,
+        pltpu.SemaphoreType.DMA,
+        pltpu.SemaphoreType.DMA,
         pltpu.SemaphoreType.DMA((2,)),
-        pltpu.SemaphoreType.DMA((2,)),
-        pltpu.SemaphoreType.DMA((nx, 2)),
-        pltpu.SemaphoreType.DMA((nx, 2)),
-        pltpu.SemaphoreType.DMA,
-        pltpu.SemaphoreType.DMA((ncopies,)),
-        pltpu.SemaphoreType.DMA((heads, nx, 2, nch)),
+        pltpu.SemaphoreType.DMA((heads, nx - 1, nch)),
+        pltpu.SemaphoreType.DMA((nx,)),
     ]
     return pl.pallas_call(
         functools.partial(kernel, ny=ny, nz=nz, nx=nx, nch=nch),

time: 59.6 us -> 53.5 us (0.90)
  Pallas kernels: 58.8 us -> 52.6 us
    pallas_call x1, Pallas kernels: 58.8 us -> 52.6 us  [on_device(): pl.pallas_call(functools.partial(kernel, ny=ny, nz=nz, nx=nx, nch=nch), o...]
where the time goes in v3:
time: 53.5 us; the launch traced here: 53.4 us
  Pallas kernels  52.6 us (98%)
  local copies, waits for them, and re-layouts  0.71 us (1%)
    pallas_call x1, Pallas kernels, on_device(): pl.pallas_call(functools.partial(kernel, ny=ny, nz=nz, nx=nx, nch=nch), o...  52.6 us

profile of v3, /device:TPU:1, one launch (start us, length us, event | category | flops | bytes accessed | tf_op | source)
XLA Modules:
  0.0 53.4 jit_solution(5436051652137622101)
XLA Ops:
  0.0 52.6 %vq_layer.1 = bf16[512,256]{1,0:T(8,128)(2,1)S(1)} custom-call(bf16[1024,128]{1,0:T(8,128)(2,1)} %bitcast.3, bf16[1024,128]{1,0:T(8,128)(2,1)} %bitcast.4, s32[2,512]{1,0:T(2,128)} %bitcast.5, bf16[2,512,128]{2,1,0:T(8,128)(2,1)} %book_ref.1, bf16[256,2048]{1,0:T(8,128)(2,1)} %w_ref.1), custom_call_target="tpu_custom_call" | custom-call | tf_op jit(solution)/shard_map/vq_layer/pallas_call | solution.py:415
  52.6 0.7 %copy.7 = bf16[512,256]{1,0:T(8,128)(2,1)} copy(bf16[512,256]{1,0:T(8,128)(2,1)S(1)} %vq_layer.1) | data formatting | bytes 524288

commit v4 on v3

--- a/solution.py
+++ b/solution.py
@@ -37,7 +37,7 @@
 def kernel(
     q_ref, v_ref, row_ref, book_ref, w_ref, out_ref,
     qin, vin, codes, book, split, vals, qs,
-    sums, raw, tot_s, tot_r, pre_s, cache,
+    sums, theirs, gsum, raw, tot_s, tot_r, pre_s, cache,
     csums, craw, ctot_s, ctot_r, cpre_s, ccache,
     code_sc, fw, aloc, stat, gath, wcol, acc,
     in_sem, z_send, z_recv, y_send, y_recv, w_send, w_recv, w_local, g_send, g_recv, g_other,
@@ -58,6 +58,18 @@
 
     def x_at(d):
         return lax.rem(x + d, nx)
+
+    npair = nz // 2
+    odd, pair = lax.rem(z, 2), z // 2
+    partner = z + 1 - 2 * odd
+
+    def slice_of(at):
+        return lax.rem(at, 2) * npair + at // 2
+
+    def far_pair(j):
+        step = (j + 1) // 2
+        sign = 1 - 2 * lax.rem(j, 2)
+        return lax.rem(pair + npair // 2 + sign * step + npair, npair)
 
     barrier = pltpu.get_barrier_semaphore()
 
@@ -122,45 +134,68 @@
     with scope("barrier"):
         pl.semaphore_wait(barrier, nz - 1 + ny - 1 + len(peers))
 
-    def z_push(source, target, chunk):
+    def z_copy(source, target, chunk, there):
+        return pltpu.make_async_remote_copy(
+            src_ref=source,
+            dst_ref=target,
+            send_sem=z_send.at[chunk],
+            recv_sem=z_recv.at[chunk],
+            device_id={"z": there},
+            device_id_type=MESH,
+        )
+
+    def push_counts():
         def push(j, carry):
             there = far_first(j)
-            pltpu.make_async_remote_copy(
-                src_ref=source.at[there],
-                dst_ref=target.at[z],
-                send_sem=z_send.at[chunk],
-                recv_sem=z_recv.at[chunk],
-                device_id={"z": there},
-                device_id_type=MESH,
-            ).start()
+            z_copy(csums.at[slice_of(there)], craw.at[z], 0, there).start()
             return carry
 
         lax.fori_loop(0, nz - 1, push, 0)
-        target[z] = source[z]
-
-    def z_push_band(source, target, chunk, start, count):
+        craw[z] = csums[slice_of(z)]
+
+    def push_counts_back():
+        def push(j, carry):
+            there = far_first(j)
+            z_copy(cpre_s.at[there], ccache.at[slice_of(z)], 3, there).start()
+            return carry
+
+        lax.fori_loop(0, nz - 1, push, 0)
+        ccache[slice_of(z)] = cpre_s[z]
+
+    def push_pair_sums(h):
+        def push(j, carry):
+            there = far_pair(j)
+            z_copy(gsum.at[h, there], raw.at[h, pair], 1 + h, 2 * there + odd).start()
+            return carry
+
+        lax.fori_loop(0, npair - 1, push, 0)
+        raw[h, pair] = gsum[h, pair]
+
+    def z_push_band(h, start, count):
         def push(j, carry):
             there = start + lax.rem(z + j, count)
 
             @pl.when(there != z)
             def _():
-                pltpu.make_async_remote_copy(
-                    src_ref=source.at[there],
-                    dst_ref=target.at[z],
-                    send_sem=z_send.at[chunk],
-                    recv_sem=z_recv.at[chunk],
-                    device_id={"z": there},
-                    device_id_type=MESH,
-                ).start()
+                z_copy(pre_s.at[h, there // 2], cache.at[h, slice_of(z)], 4 + h, there).start()
 
             return carry
 
         lax.fori_loop(0, count, push, 0)
 
+    def half_rows(ref, h, which):
+        return ref.at[h, pl.ds(which * npair, npair)]
+
+    def swap(h):
+        return z_copy(half_rows(sums, h, 1 - odd), half_rows(theirs, h, 1 - odd), 6 + h, partner)
+
+    def fill(h):
+        return z_copy(half_rows(sums, h, 0), half_rows(theirs, h, 0), 8 + h, partner)
+
     with scope("push_raw"):
-        z_push(csums, craw, 0)
+        push_counts()
         for h in range(heads):
-            z_push(sums.at[h], raw.at[h], 1 + h)
+            swap(h).start()
 
     def w_slice(dx, dc):
         owner = x_at(dx) * 2 + lax.rem(c + dc, 2)
@@ -186,16 +221,34 @@
             qs[h] = split[pl.ds(h, tokens, stride=heads), :].astype(BF16)
             block_scores(h)
 
+    for h in range(heads):
+        with scope(f"wait_swap{h}"):
+            wait_bytes(half_rows(theirs, h, odd), z_recv.at[6 + h])
+        own = half_rows(sums, h, odd)[...].astype(F32)
+        gsum[h] = (own + half_rows(theirs, h, odd)[...].astype(F32)).astype(BF16)
+        push_pair_sums(h)
+
+    @pl.when(odd == 0)
+    def _():
+        for h in range(heads):
+            fill(h).start()
+
+    def y_copy(source, target, chunk, d):
+        return pltpu.make_async_remote_copy(
+            src_ref=source,
+            dst_ref=target.at[d],
+            send_sem=y_send.at[chunk, d - 1],
+            recv_sem=y_recv.at[chunk, d - 1],
+            device_id={"y": lax.rem(y + d, ny)},
+            device_id_type=MESH,
+        )
+
     def y_push(source, target, chunk):
         for d in range(1, ny):
-            pltpu.make_async_remote_copy(
-                src_ref=source,
-                dst_ref=target.at[ny - d],
-                send_sem=y_send.at[chunk],
-                recv_sem=y_recv.at[chunk],
-                device_id={"y": lax.rem(y + d, ny)},
-                device_id_type=MESH,
-            ).start()
+
+            @pl.when(y + d < ny)
+            def _(d=d):
+                y_copy(source, target, chunk, d).start()
 
     with scope("wait_craw"):
         wait_bytes(craw.at[pl.ds(0, nz - 1)], z_recv.at[0])
@@ -207,45 +260,48 @@
     y_push(ctot_s, ctot_r, 0)
     def row_total(h):
         with scope(f"wait_raw{h}"):
-            wait_bytes(raw.at[h, pl.ds(0, nz - 1)], z_recv.at[1 + h])
+            wait_bytes(raw.at[h, pl.ds(0, npair - 1)], z_recv.at[1 + h])
         so_far = raw[h, 0].astype(F32)
-        for n in range(1, nz):
+        for n in range(1, npair):
             so_far = so_far + raw[h, n].astype(F32)
         tot_s[h] = so_far.astype(BF16)
         y_push(tot_s.at[h], tot_r.at[h], 1 + h)
 
-    def earlier_rows(target):
+    def earlier_rows(source, target, chunk):
         total = None
         for d in range(1, ny):
-            row = jnp.where(y + d >= ny, target[d].astype(F32), 0.0)
+
+            @pl.when(y >= d)
+            def _(d=d):
+                y_copy(source, target, chunk, d).wait_recv()
+
+            row = jnp.where(y >= d, target[d].astype(F32), 0.0)
             total = row if total is None else total + row
         return total
 
     def send_prefix(h):
         with scope(f"wait_y{h}"):
-            wait_bytes(tot_r.at[h, pl.ds(1, ny - 1)], y_recv.at[1 + h])
+            so_far = earlier_rows(tot_s.at[h], tot_r.at[h], 1 + h)
         with scope(f"prefix{h}"):
-            so_far = earlier_rows(tot_r.at[h])
-            for n in range(nz):
+            for n in range(npair):
                 pre_s[h, n] = so_far.astype(BF16)
                 so_far = so_far + raw[h, n].astype(F32)
-            cache[h, z] = pre_s[h, z]
-            z_push_band(pre_s.at[h], cache.at[h], 4 + h, 0, nz // 4)
-            z_push_band(pre_s.at[h], cache.at[h], 4 + h, nz // 4, nz // 4)
+            cache[h, slice_of(z)] = pre_s[h, pair]
+            z_push_band(h, 0, nz // 4)
+            z_push_band(h, nz // 4, nz // 4)
 
     row_total(0)
     with scope("wait_cy"):
-        wait_bytes(ctot_r.at[pl.ds(1, ny - 1)], y_recv.at[0])
-    above = earlier_rows(ctot_r)
+        above = earlier_rows(ctot_s, ctot_r, 0)
     for n in range(nz):
         cpre_s[n] = cbefore[n] + above
-    z_push(cpre_s, ccache, 3)
+    push_counts_back()
     for h in range(1, heads):
         row_total(h)
     for h in range(heads):
         send_prefix(h)
     for h in range(heads):
-        z_push_band(pre_s.at[h], cache.at[h], 4 + h, nz // 2, nz // 2)
+        z_push_band(h, nz // 2, nz // 2)
 
     with scope("wait_ccache"):
         wait_bytes(ccache.at[pl.ds(0, nz - 1)], z_recv.at[3])
@@ -275,7 +331,7 @@
     right, left = 1, nx - 1
 
     def piece(slot, h, r):
-        return gath.at[slot[0], slot[1], pl.ds(r * part, part), pl.ds(h * width, width)]
+        return gath.at[slot[0], slot[1], h, pl.ds(r * part, part)]
 
     def arrival(h, r, slot):
         return g_other.at[slot[0]] if slot[1] else g_recv.at[h, slot[0] - 1, r]
@@ -298,8 +354,14 @@
     def finish(h):
         with scope(f"wait_cache{h}"):
             wait_bytes(cache.at[h, pl.ds(0, nz - 1)], z_recv.at[4 + h])
-        table = cache[h].reshape(ncodes, width)
-        gath[0, 0, :, h * width : (h + 1) * width] = (aloc[h] + dot_nn(fw[h], table)).astype(BF16)
+
+        @pl.when(odd == 1)
+        def _():
+            fill(h).wait_recv()
+
+        mine = jnp.where(odd == 1, theirs[h].astype(F32), 0.0)
+        table = (cache[h].astype(F32) + mine).astype(BF16).reshape(ncodes, width)
+        gath[0, 0, h] = (aloc[h] + dot_nn(fw[h], table)).astype(BF16)
         for r, s in zip((*low, *high), (*high, *low), strict=True):
             send(h, r, (0, 0), right, 0)
             send(h, s, (0, 0), left, 0)
@@ -330,7 +392,8 @@
                 send(h, s, (2, 0), 0, 1)
 
     def project(slot, first=False):
-        add = dot_nn(gath[slot[0], slot[1]], wcol[slot[0] * 2 + slot[1]])
+        rows = jnp.concatenate([gath[slot[0], slot[1], h] for h in range(heads)], axis=1)
+        add = dot_nn(rows, wcol[slot[0] * 2 + slot[1]])
         acc[...] = add if first else acc[...] + add
 
     finish(0)
@@ -357,12 +420,27 @@
     with scope("tail"):
         wait_bytes(gath.at[pl.ds(0, 3), 0], g_send.at[0])
         wait_bytes(gath.at[pl.ds(0, nx), 0], g_send.at[1])
-        for chunk, ref in ((0, csums), (1, sums.at[0]), (2, sums.at[1])):
+        for chunk, ref in ((0, csums), (3, csums), (4, cache.at[0]), (5, cache.at[1])):
             wait_bytes(ref.at[pl.ds(0, nz - 1)], z_send.at[chunk])
-        for chunk, ref in ((3, cpre_s), (4, pre_s.at[0]), (5, pre_s.at[1])):
-            wait_bytes(ref.at[pl.ds(0, nz - 1)], z_send.at[chunk])
-        for chunk, ref in ((0, ctot_r), (1, tot_r.at[0]), (2, tot_r.at[1])):
-            wait_bytes(ref.at[pl.ds(1, ny - 1)], y_send.at[chunk])
+        for h in range(heads):
+            wait_bytes(raw.at[h, pl.ds(0, npair - 1)], z_send.at[1 + h])
+            swap(h).wait_send()
+
+        @pl.when(odd == 0)
+        def _():
+            for h in range(heads):
+                fill(h).wait_send()
+
+        for chunk, source, target in (
+            (0, ctot_s, ctot_r),
+            (1, tot_s.at[0], tot_r.at[0]),
+            (2, tot_s.at[1], tot_r.at[1]),
+        ):
+            for d in range(1, ny):
+
+                @pl.when(y + d < ny)
+                def _(chunk=chunk, source=source, target=target, d=d):
+                    y_copy(source, target, chunk, d).wait_send()
 
 
 def on_device(queries, values, codes, codebook, out_weight, *, ny, nz, nx):
@@ -383,9 +461,11 @@
         pltpu.VMEM((heads, tokens, width), BF16),
         pltpu.VMEM((heads, nz, sl, width), BF16),
         pltpu.VMEM((heads, nz, sl, width), BF16),
+        pltpu.VMEM((heads, nz // 2, sl, width), BF16),
+        pltpu.VMEM((heads, nz // 2, sl, width), BF16),
         pltpu.VMEM((heads, sl, width), BF16),
         pltpu.VMEM((heads, ny, sl, width), BF16),
-        pltpu.VMEM((heads, nz, sl, width), BF16),
+        pltpu.VMEM((heads, nz // 2, sl, width), BF16),
         pltpu.VMEM((heads, nz, sl, width), BF16),
         pltpu.VMEM((nz, 1, width), F32),
         pltpu.VMEM((nz, 1, width), F32),
@@ -397,14 +477,14 @@
         pltpu.VMEM((heads, tokens, ncodes), BF16),
         pltpu.VMEM((heads, tokens, width), F32),
         pltpu.VMEM((heads, 2, tokens, 1), F32),
-        pltpu.VMEM((nx, 2, tokens, depth), BF16),
+        pltpu.VMEM((nx, 2, heads, tokens, width), BF16),
         pltpu.VMEM((nx * 2, depth, cols), BF16),
         pltpu.VMEM((tokens, cols), F32),
         pltpu.SemaphoreType.DMA((4,)),
-        pltpu.SemaphoreType.DMA((6,)),
-        pltpu.SemaphoreType.DMA((6,)),
-        pltpu.SemaphoreType.DMA((3,)),
-        pltpu.SemaphoreType.DMA((3,)),
+        pltpu.SemaphoreType.DMA((10,)),
+        pltpu.SemaphoreType.DMA((10,)),
+        pltpu.SemaphoreType.DMA((3, ny - 1)),
+        pltpu.SemaphoreType.DMA((3, ny - 1)),
         pltpu.SemaphoreType.DMA,
         pltpu.SemaphoreType.DMA,
         pltpu.SemaphoreType.DMA,

time: 53.5 us -> 52.9 us (0.989)
  the two profiles are of different devices: /device:TPU:1 before, /device:TPU:57 now
where the time goes in v4:
time: 52.9 us; the launch traced here: 52.8 us
  Pallas kernels  52.1 us (98%)
  local copies, waits for them, and re-layouts  0.71 us (1%)
    pallas_call x1, Pallas kernels, on_device(): pl.pallas_call(functools.partial(kernel, ny=ny, nz=nz, nx=nx, nch=nch), o...  52.1 us

profile of v4, /device:TPU:57, one launch (start us, length us, event | category | flops | bytes accessed | tf_op | source)
XLA Modules:
  0.0 52.8 jit_solution(1837570554493715741)
XLA Ops:
  0.0 52.1 %vq_layer.1 = bf16[512,256]{1,0:T(8,128)(2,1)S(1)} custom-call(bf16[1024,128]{1,0:T(8,128)(2,1)} %bitcast.3, bf16[1024,128]{1,0:T(8,128)(2,1)} %bitcast.4, s32[2,512]{1,0:T(2,128)} %bitcast.5, bf16[2,512,128]{2,1,0:T(8,128)(2,1)} %book_ref.1, bf16[256,2048]{1,0:T(8,128)(2,1)} %w_ref.1), custom_call_target="tpu_custom_call" | custom-call | tf_op jit(solution)/shard_map/vq_layer/pallas_call | solution.py:495
  52.1 0.7 %copy.7 = bf16[512,256]{1,0:T(8,128)(2,1)} copy(bf16[512,256]{1,0:T(8,128)(2,1)S(1)} %vq_layer.1) | data formatting | bytes 524288

commit v5 on v4

--- a/solution.py
+++ b/solution.py
@@ -40,7 +40,7 @@
     sums, theirs, gsum, raw, tot_s, tot_r, pre_s, cache,
     csums, craw, ctot_s, ctot_r, cpre_s, ccache,
     code_sc, fw, aloc, stat, gath, wcol, acc,
-    in_sem, z_send, z_recv, y_send, y_recv, w_send, w_recv, w_local, g_send, g_recv, g_other,
+    in_sem, z_send, z_recv, y_send, y_recv, w_send, w_recv, w_local, g_send, g_recv, g_slot,
     *, ny, nz, nx, nch,
 ):
     heads, ncodes, width = book_ref.shape
@@ -328,30 +328,33 @@
         for h in range(heads):
             code_weights(h)
 
-    right, left = 1, nx - 1
+    right, left, beyond = 1, nx - 1, 2
+    low, high = range(nch // 2), range(nch // 2, nch)
 
     def piece(slot, h, r):
-        return gath.at[slot[0], slot[1], h, pl.ds(r * part, part)]
-
-    def arrival(h, r, slot):
-        return g_other.at[slot[0]] if slot[1] else g_recv.at[h, slot[0] - 1, r]
-
-    def send(h, r, slot, dx, dc):
+        return gath.at[slot[0] * 2 + slot[1], h, pl.ds(r * part, part)]
+
+    def send(h, r, slot, dx, dc, whole=False):
         there = ((slot[0] - dx) % nx, (slot[1] + dc) % 2)
+        number = there[0] * 2 + there[1]
         pltpu.make_async_remote_copy(
             src_ref=piece(slot, h, r),
             dst_ref=piece(there, h, r),
-            send_sem=g_send.at[1 if dc else 0],
-            recv_sem=arrival(h, r, there),
+            send_sem=g_send.at[0 if dx else 1],
+            recv_sem=g_slot.at[number] if whole else g_recv.at[number - 2, h, r],
             device_id={"x": x_at(dx), "c": lax.rem(c + dc, 2)},
             device_id_type=MESH,
         ).start()
 
     def landed(h, r, slot):
-        wait_bytes(piece(slot, h, r), arrival(h, r, slot))
-
-    low, high = range(nch // 2), range(nch // 2, nch)
-    def finish(h):
+        wait_bytes(piece(slot, h, r), g_recv.at[slot[0] * 2 + slot[1] - 2, h, r])
+
+    def landed_whole(slot):
+        number = slot[0] * 2 + slot[1]
+        with scope("slot"):
+            wait_bytes(gath.at[number], g_slot.at[number])
+
+    def own_rows(h, dc):
         with scope(f"wait_cache{h}"):
             wait_bytes(cache.at[h, pl.ds(0, nz - 1)], z_recv.at[4 + h])
 
@@ -361,65 +364,87 @@
 
         mine = jnp.where(odd == 1, theirs[h].astype(F32), 0.0)
         table = (cache[h].astype(F32) + mine).astype(BF16).reshape(ncodes, width)
-        gath[0, 0, h] = (aloc[h] + dot_nn(fw[h], table)).astype(BF16)
+        gath[0, h] = (aloc[h] + dot_nn(fw[h], table)).astype(BF16)
         for r, s in zip((*low, *high), (*high, *low), strict=True):
-            send(h, r, (0, 0), right, 0)
-            send(h, s, (0, 0), left, 0)
+            send(h, r, (0, 0), right, dc)
+            send(h, s, (0, 0), left, dc)
         for r in range(nch):
-            send(h, r, (0, 0), 0, 1)
-
-    def relay(h):
-        with scope(f"relay{h}"):
-            for r, s in zip(low, high, strict=True):
-                landed(h, r, (left, 0))
-                send(h, r, (left, 0), right, 0)
-                send(h, r, (left, 0), 0, 1)
-                landed(h, s, (right, 0))
-                send(h, s, (right, 0), left, 0)
-                send(h, s, (right, 0), 0, 1)
-            for r, s in zip(high, low, strict=True):
-                landed(h, r, (left, 0))
-                send(h, r, (left, 0), 0, 1)
-                landed(h, s, (right, 0))
-                send(h, s, (right, 0), 0, 1)
-
-    def across(h):
-        with scope(f"across{h}"):
-            for r, s in zip(low, high, strict=True):
-                landed(h, r, (2, 0))
-                send(h, r, (2, 0), 0, 1)
-                landed(h, s, (2, 0))
-                send(h, s, (2, 0), 0, 1)
+            send(h, r, (0, 0), 0, 1, True)
 
     def project(slot, first=False):
-        rows = jnp.concatenate([gath[slot[0], slot[1], h] for h in range(heads)], axis=1)
-        add = dot_nn(rows, wcol[slot[0] * 2 + slot[1]])
+        number = slot[0] * 2 + slot[1]
+        rows = jnp.concatenate([gath[number, h] for h in range(heads)], axis=1)
+        add = dot_nn(rows, wcol[number])
         acc[...] = add if first else acc[...] + add
 
-    finish(0)
-    finish(1)
-    with scope("wait_w"):
-        own_w.wait()
-        w_all = wcol.at[pl.ds(1, len(peers))]
-        wait_bytes(w_all, w_recv)
-        wait_bytes(w_all, w_send)
-    project((0, 0), True)
-    relay(0)
-    relay(1)
-    for slot in ((left, 0), (right, 0)):
-        project(slot)
-    across(0)
-    across(1)
-    for slot in ((2, 0), (0, 1), (left, 1), (right, 1), (2, 1)):
-        if slot[1]:
-            with scope("other"):
-                wait_bytes(gath.at[slot[0], slot[1]], g_other.at[slot[0]])
-        project(slot)
-    out_ref[...] = acc[...].astype(BF16)
+    def weights_in():
+        with scope("wait_w"):
+            own_w.wait()
+            w_all = wcol.at[pl.ds(1, len(peers))]
+            wait_bytes(w_all, w_recv)
+            wait_bytes(w_all, w_send)
+
+    @pl.when(c == 0)
+    def _():
+        for h in range(heads):
+            own_rows(h, 1)
+        weights_in()
+        project((0, 0), True)
+        for slot in ((0, 1), (left, 1), (right, 1), (beyond, 1), (left, 0), (right, 0), (beyond, 0)):
+            landed_whole(slot)
+            project(slot)
+        out_ref[...] = acc[...].astype(BF16)
+        wait_bytes(gath.at[pl.ds(0, 2)], g_send.at[0])
+        wait_bytes(gath.at[0], g_send.at[1])
+
+    @pl.when(c == 1)
+    def _():
+        def relay(h, sc):
+            with scope(f"relay{h}{sc}"):
+                for r, s in zip(low, high, strict=True):
+                    landed(h, r, (left, sc))
+                    send(h, r, (left, sc), right, 0)
+                    send(h, r, (left, sc), 0, 1, True)
+                    landed(h, s, (right, sc))
+                    send(h, s, (right, sc), left, 0)
+                    send(h, s, (right, sc), 0, 1, True)
+                for r, s in zip(high, low, strict=True):
+                    landed(h, r, (left, sc))
+                    send(h, r, (left, sc), 0, 1, True)
+                    landed(h, s, (right, sc))
+                    send(h, s, (right, sc), 0, 1, True)
+
+        def across(h, sc):
+            with scope(f"across{h}{sc}"):
+                for pair_of in zip(low, high, strict=True):
+                    for r in pair_of:
+                        landed(h, r, (beyond, sc))
+                        send(h, r, (beyond, sc), 0, 1, True)
+
+        own_rows(0, 0)
+        own_rows(1, 0)
+        weights_in()
+        relay(0, 0)
+        relay(1, 0)
+        across(0, 0)
+        project((0, 0), True)
+        relay(0, 1)
+        across(1, 0)
+        project((left, 0))
+        project((right, 0))
+        relay(1, 1)
+        across(0, 1)
+        landed_whole((0, 1))
+        project((0, 1))
+        project((beyond, 0))
+        across(1, 1)
+        for slot in ((left, 1), (right, 1), (beyond, 1)):
+            project(slot)
+        out_ref[...] = acc[...].astype(BF16)
+        wait_bytes(gath.at[pl.ds(0, 4)], g_send.at[0])
+        wait_bytes(gath.at[pl.ds(0, 7)], g_send.at[1])
 
     with scope("tail"):
-        wait_bytes(gath.at[pl.ds(0, 3), 0], g_send.at[0])
-        wait_bytes(gath.at[pl.ds(0, nx), 0], g_send.at[1])
         for chunk, ref in ((0, csums), (3, csums), (4, cache.at[0]), (5, cache.at[1])):
             wait_bytes(ref.at[pl.ds(0, nz - 1)], z_send.at[chunk])
         for h in range(heads):
@@ -477,7 +502,7 @@
         pltpu.VMEM((heads, tokens, ncodes), BF16),
         pltpu.VMEM((heads, tokens, width), F32),
         pltpu.VMEM((heads, 2, tokens, 1), F32),
-        pltpu.VMEM((nx, 2, heads, tokens, width), BF16),
+        pltpu.VMEM((nx * 2, heads, tokens, width), BF16),
         pltpu.VMEM((nx * 2, depth, cols), BF16),
         pltpu.VMEM((tokens, cols), F32),
         pltpu.SemaphoreType.DMA((4,)),
@@ -489,8 +514,8 @@
         pltpu.SemaphoreType.DMA,
         pltpu.SemaphoreType.DMA,
         pltpu.SemaphoreType.DMA((2,)),
-        pltpu.SemaphoreType.DMA((heads, nx - 1, nch)),
-        pltpu.SemaphoreType.DMA((nx,)),
+        pltpu.SemaphoreType.DMA((nx * 2 - 2, heads, nch)),
+        pltpu.SemaphoreType.DMA((nx * 2,)),
     ]
     return pl.pallas_call(
         functools.partial(kernel, ny=ny, nz=nz, nx=nx, nch=nch),

time: 52.9 us -> 51.9 us (0.981)
  Pallas kernels: 52.1 us -> 51.1 us
    pallas_call x1, Pallas kernels: 52.1 us -> 51.1 us  [on_device(): pl.pallas_call(functools.partial(kernel, ny=ny, nz=nz, nx=nx, nch=nch), o...]
where the time goes in v5:
time: 51.9 us; the launch traced here: 51.8 us
  Pallas kernels  51.1 us (98%)
  local copies, waits for them, and re-layouts  0.71 us (1%)
    pallas_call x1, Pallas kernels, on_device(): pl.pallas_call(functools.partial(kernel, ny=ny, nz=nz, nx=nx, nch=nch), o...  51.1 us

profile of v5, /device:TPU:57, one launch (start us, length us, event | category | flops | bytes accessed | tf_op | source)
XLA Modules:
  0.0 51.8 jit_solution(14989178030511122917)
XLA Ops:
  0.0 51.1 %vq_layer.1 = bf16[512,256]{1,0:T(8,128)(2,1)S(1)} custom-call(bf16[1024,128]{1,0:T(8,128)(2,1)} %bitcast.3, bf16[1024,128]{1,0:T(8,128)(2,1)} %bitcast.4, s32[2,512]{1,0:T(2,128)} %bitcast.5, bf16[2,512,128]{2,1,0:T(8,128)(2,1)} %book_ref.1, bf16[256,2048]{1,0:T(8,128)(2,1)} %w_ref.1), custom_call_target="tpu_custom_call" | custom-call | tf_op jit(solution)/shard_map/vq_layer/pallas_call | solution.py:520
  51.1 0.7 %copy.7 = bf16[512,256]{1,0:T(8,128)(2,1)} copy(bf16[512,256]{1,0:T(8,128)(2,1)S(1)} %vq_layer.1) | data formatting | bytes 524288

commit v6 on v5

--- a/solution.py
+++ b/solution.py
@@ -288,7 +288,6 @@
                 so_far = so_far + raw[h, n].astype(F32)
             cache[h, slice_of(z)] = pre_s[h, pair]
             z_push_band(h, 0, nz // 4)
-            z_push_band(h, nz // 4, nz // 4)
 
     row_total(0)
     with scope("wait_cy"):
@@ -300,8 +299,9 @@
         row_total(h)
     for h in range(heads):
         send_prefix(h)
-    for h in range(heads):
-        z_push_band(h, nz // 2, nz // 2)
+    for start, count in ((nz // 4, nz // 4), (nz // 2, nz // 2)):
+        for h in range(heads):
+            z_push_band(h, start, count)
 
     with scope("wait_ccache"):
         wait_bytes(ccache.at[pl.ds(0, nz - 1)], z_recv.at[3])

time: 51.9 us -> 50.5 us (0.973)
  the two profiles are of different devices: /device:TPU:57 before, /device:TPU:1 now
where the time goes in v6:
time: 50.5 us; the launch traced here: 50.3 us
  Pallas kernels  49.6 us (98%)
  local copies, waits for them, and re-layouts  0.71 us (1%)
    pallas_call x1, Pallas kernels, on_device(): pl.pallas_call(functools.partial(kernel, ny=ny, nz=nz, nx=nx, nch=nch), o...  49.6 us

profile of v6, /device:TPU:1, one launch (start us, length us, event | category | flops | bytes accessed | tf_op | source)
XLA Modules:
  0.0 50.3 jit_solution(3118960191136498548)
XLA Ops:
  0.0 49.6 %vq_layer.1 = bf16[512,256]{1,0:T(8,128)(2,1)S(1)} custom-call(bf16[1024,128]{1,0:T(8,128)(2,1)} %bitcast.3, bf16[1024,128]{1,0:T(8,128)(2,1)} %bitcast.4, s32[2,512]{1,0:T(2,128)} %bitcast.5, bf16[2,512,128]{2,1,0:T(8,128)(2,1)} %book_ref.1, bf16[256,2048]{1,0:T(8,128)(2,1)} %w_ref.1), custom_call_target="tpu_custom_call" | custom-call | tf_op jit(solution)/shard_map/vq_layer/pallas_call | solution.py:520
  49.6 0.7 %copy.7 = bf16[512,256]{1,0:T(8,128)(2,1)} copy(bf16[512,256]{1,0:T(8,128)(2,1)S(1)} %vq_layer.1) | data formatting | bytes 524288

commit v7 on v6

--- a/solution.py
+++ b/solution.py
@@ -436,10 +436,10 @@
         across(0, 1)
         landed_whole((0, 1))
         project((0, 1))
-        project((beyond, 0))
+        for slot in ((beyond, 0), (left, 1), (right, 1)):
+            project(slot)
         across(1, 1)
-        for slot in ((left, 1), (right, 1), (beyond, 1)):
-            project(slot)
+        project((beyond, 1))
         out_ref[...] = acc[...].astype(BF16)
         wait_bytes(gath.at[pl.ds(0, 4)], g_send.at[0])
         wait_bytes(gath.at[pl.ds(0, 7)], g_send.at[1])

time: 50.5 us -> 50.5 us (level)
  no operation moved by 1% of the time
where the time goes in v7:
time: 50.5 us; the launch traced here: 50.3 us
  Pallas kernels  49.6 us (98%)
  local copies, waits for them, and re-layouts  0.71 us (1%)
    pallas_call x1, Pallas kernels, on_device(): pl.pallas_call(functools.partial(kernel, ny=ny, nz=nz, nx=nx, nch=nch), o...  49.6 us

profile of v7, /device:TPU:1, one launch (start us, length us, event | category | flops | bytes accessed | tf_op | source)
XLA Modules:
  0.0 50.3 jit_solution(12131359033064248329)
XLA Ops:
  0.0 49.6 %vq_layer.1 = bf16[512,256]{1,0:T(8,128)(2,1)S(1)} custom-call(bf16[1024,128]{1,0:T(8,128)(2,1)} %bitcast.3, bf16[1024,128]{1,0:T(8,128)(2,1)} %bitcast.4, s32[2,512]{1,0:T(2,128)} %bitcast.5, bf16[2,512,128]{2,1,0:T(8,128)(2,1)} %book_ref.1, bf16[256,2048]{1,0:T(8,128)(2,1)} %w_ref.1), custom_call_target="tpu_custom_call" | custom-call | tf_op jit(solution)/shard_map/vq_layer/pallas_call | solution.py:520
  49.6 0.7 %copy.7 = bf16[512,256]{1,0:T(8,128)(2,1)} copy(bf16[512,256]{1,0:T(8,128)(2,1)S(1)} %vq_layer.1) | data formatting | bytes 524288
